TPU v7x, 32 devices: a whole 2x2x4 slice. The times are simulated.
32 devices in a mesh: comp: 2 (over core), blk: 16 (over z, y, x).
Axes of the slice: x: 2, y: 2, z: 4, core: 2. Of those that a mesh axis runs over, the one named last changes fastest.
Arguments:
- initial: float32 [2, 5, 128, 2048], P('comp', None, 'blk'), may hold values from -3 to 3
- ice_forcing: float32 [5, 128, 2048], P(None, 'blk'), may hold values from -2 to 4, as said below
- ocean_current: float32 [2, 128, 2048], P(None, 'blk'), may hold values from -1 to 1
- ice_cover: int32 [128, 2048], P('blk'), may hold values from 0 to 1, as said below
- targets: int32 [2, 128, 2048], P(None, 'blk'), may hold values from 0 to 32767, as said below
- weights: int32 [2, 128, 2048], P(None, 'blk'), may hold values from 1 to 4
Outputs:
- state_out: float32 [2, 5, 128, 2048], P('comp', None, 'blk')
- coupled: float32 [2, 3, 128, 2048], P('comp', None, 'blk')
Inputs may be any that keep to these rules, and one draw needn't show every extreme that they name: `ice_forcing`: channel 0 (mass) lies in 0.5 to 4, channel 1 (strength) and channel 4 (melt rate) in 0.2 to 2, channels 2 and 3 (wind stress) in -2 to 2. `ice_cover`: the share of ice-covered cells differs from strip to strip of 8 rows. `targets`: an entry of an ice cell at row r of its strip names an ocean row of the window no earlier than r.
All inputs are finite; a program needn't handle non-finite values.
Results may differ from a plain program's by a relative error of at most 0.0003.
Values sent between devices are 32-bit elements; how exact they have to be, the bound alone decides.
A program may use at most 128 MiB of HBM per device.

v0:
```python
import functools

import jax
import jax.numpy as jnp
from jax import lax
from jax.experimental import pallas as pl
from jax.experimental.pallas import tpu as pltpu
from jax.sharding import PartitionSpec as P

SUBCYCLES = 16
MESH = pl.DeviceIdType.MESH
PAD = 128
PARTS = 2

coriolis = 0.1
inertia = 4.0
courant = 0.2
dilution = 0.5
weight_norm = 4.0
level_speed = (1.0, 0.8, 0.6, 0.45, 0.3)


def rolled(value, steps, axis):
    return pltpu.roll(value, steps % value.shape[axis], axis)


def rows_diff(value):
    return rolled(value, -1, 0) - rolled(value, 1, 0)


def chunk_width(cols):
    return 256 if cols % 256 == 0 else 128


def stress_stage(work, stat, start, width):
    wide = pl.ds(start, width + 2 * PAD)
    mid = pl.ds(start + PAD, width)
    inner = slice(PAD, PAD + width)
    vel_x, vel_y = work[0, :, wide], work[1, :, wide]
    cx = (rolled(vel_x, -1, 1) - rolled(vel_x, 1, 1))[:, inner]
    cy = (rolled(vel_y, -1, 1) - rolled(vel_y, 1, 1))[:, inner]
    rx = rows_diff(vel_x[:, inner])
    ry = rows_diff(vel_y[:, inner])
    e_d = rx + cy
    e_t = rx - cy
    e_s = cx + ry
    inv = lax.rsqrt(0.25 * (e_d * e_d) + 0.0625 * (e_t * e_t + e_s * e_s) + 0.01)
    third = stat[0, :, pl.ds(start, width)]
    scaled = third * inv
    work[2, :, mid] = work[2, :, mid] * (2.0 / 3.0) + (0.5 * scaled * e_d - third)
    work[3, :, mid] = work[3, :, mid] * (2.0 / 3.0) + 0.125 * scaled * e_t
    work[4, :, mid] = work[4, :, mid] * (2.0 / 3.0) + 0.0625 * scaled * e_s


def velocity_stage(work, stat, total, start, width, rows):
    wide = pl.ds(start, width + 2 * PAD)
    mid = pl.ds(start + PAD, width)
    here = pl.ds(start, width)
    inner = slice(PAD, PAD + width)
    shear = work[4, :, wide]
    one, two = work[2, :, wide], work[3, :, wide]
    across_shear = (rolled(shear, -1, 1) - rolled(shear, 1, 1))[:, inner]
    lower = one - two
    across_yy = (rolled(lower, -1, 1) - rolled(lower, 1, 1))[:, inner]
    force_x = rows_diff((one + two)[:, inner]) + 2.0 * across_shear
    force_y = 2.0 * rows_diff(shear[:, inner]) + across_yy
    old_x, old_y = work[0, :, mid], work[1, :, mid]
    keep, push = stat[1, :, here], stat[2, :, here]
    new_x = keep * (old_x + coriolis * old_y) + push * force_x + stat[3, :, here]
    new_y = keep * (old_y - coriolis * old_x) + push * force_y + stat[4, :, here]
    work[0, :, mid] = new_x
    work[1, :, mid] = new_y
    own_x, own_y = new_x[rows : 2 * rows], new_y[rows : 2 * rows]
    total[0, :, here] += own_x
    total[1, :, here] += own_y
    total[2, :, here] += jnp.sqrt(1.0 + own_x * own_x + own_y * own_y)


def ocean_stage(source, target, coef, start, width):
    wide = pl.ds(start, width + 2 * PAD)
    mid = pl.ds(start + PAD, width)
    here = pl.ds(start, width)
    inner = slice(PAD, PAD + width)
    up, down, east, west = (coef[i, :, here] for i in range(4))
    for level, speed in enumerate(level_speed):
        tracer = source[level, :, wide]
        centre = tracer[:, inner]
        right = rolled(tracer, -1, 1)[:, inner] - centre
        left = centre - rolled(tracer, 1, 1)[:, inner]
        above = rolled(centre, -1, 0) - centre
        below = centre - rolled(centre, 1, 0)
        change = up * below + down * above + east * left + west * right
        target[level, :, mid] = centre - speed * change


def turns_kernel(
    initial_in, forcing_in, current_in, cover_in, state, average,
    initial, forcing, current, cover,
    own, own_stat, halo, halo_stat, work, spare, stat, total, mean,
    load, near_send, near_recv, far_send, far_recv,
    stat_near_send, stat_near_recv, stat_far_send, stat_far_recv,
    mean_send, mean_recv, go,
):
    me = lax.axis_index("blk")
    comp = lax.axis_index("comp")
    count = lax.axis_size("blk")
    fields, rows, cols = initial.shape
    width = chunk_width(cols)
    chunks = cols // width
    near = 1 - lax.rem(me, 2)
    far = 1 - near
    partner = me + 2 * near - 1
    relay_to = me + 4 * near - 2
    relay_from = me - 4 * near + 2
    can_send = jnp.logical_and(relay_to >= 0, relay_to < count)
    can_recv = jnp.logical_and(relay_from >= 0, relay_from < count)
    relay_to = lax.rem(relay_to + count, count)
    relay_from = lax.rem(relay_from + count, count)

    barrier = pltpu.get_barrier_semaphore()

    def greet(where):
        pl.semaphore_signal(barrier, inc=1, device_id=where, device_id_type=MESH)

    greet({"blk": partner})
    greet({"comp": 1 - comp})
    pl.when(can_send)(lambda: greet({"blk": relay_to}))
    pl.when(can_recv)(lambda: greet({"blk": relay_from}))
    loads = [
        pltpu.make_async_copy(source, target, load.at[i])
        for i, (source, target) in enumerate(
            (
                (initial_in, initial),
                (current_in, current),
                (forcing_in, forcing),
                (cover_in, cover),
            )
        )
    ]
    for copy in loads:
        copy.start()

    work[...] = jnp.zeros_like(work)
    total[...] = jnp.zeros_like(total)

    def enter():
        pl.semaphore_wait(barrier, 2 + can_send.astype(jnp.int32) + can_recv.astype(jnp.int32))

    def copies(source, target, pieces, near_sems, far_sems):
        first, second = [], []
        wide = cols // PARTS
        for index in range(pieces * PARTS):
            piece, place = index // PARTS, pl.ds(index % PARTS * wide, wide)
            first.append(
                pltpu.make_async_remote_copy(
                    source.at[piece, :, place], target.at[far, piece, :, place],
                    near_sems[0].at[index], near_sems[1].at[index],
                    device_id={"blk": partner}, device_id_type=MESH,
                )
            )
            second.append(
                pltpu.make_async_remote_copy(
                    target.at[near, piece, :, place], target.at[far, piece, :, place],
                    far_sems[0].at[index], far_sems[1].at[index],
                    device_id={"blk": relay_to}, device_id_type=MESH,
                )
            )
        return first, second

    def start(pair):
        for copy in pair[0]:
            copy.start()

    def relay(pair):
        for first, second in zip(*pair):
            first.wait_recv()
            pl.when(can_send)(second.start)

    def arrive(pair):
        @pl.when(can_recv)
        def _():
            for copy in pair[1]:
                copy.wait_recv()

    def sent(pair):
        for copy in pair[0]:
            copy.wait_send()

        @pl.when(can_send)
        def _():
            for copy in pair[1]:
                copy.wait_send()

    def clear_edges(turns):
        @pl.when(jnp.logical_not(can_recv))
        def _():
            halo_stat[far] = jnp.zeros(halo_stat.shape[1:], jnp.float32)
            for turn in range(turns):
                halo[turn, far] = jnp.zeros(halo.shape[2:], jnp.float32)

    inside = slice(PAD, PAD + cols)

    def fill_own(source):
        for field in range(fields):
            work[field, rows : 2 * rows, inside] = source[field]

    def fill_sides(turn):
        for field in range(fields):
            work[field, 0:rows, inside] = halo[turn, 0, field]
            work[field, 2 * rows : 3 * rows, inside] = halo[turn, 1, field]

    def exchange_of(turn, source):
        return copies(
            source, halo.at[turn], fields,
            (near_send.at[turn], near_recv.at[turn]), (far_send.at[turn], far_recv.at[turn]),
        )

    def stats_of(source, pieces):
        return copies(
            source, halo_stat, pieces,
            (stat_near_send, stat_near_recv), (stat_far_send, stat_far_recv),
        )

    mean_copy = pltpu.make_async_remote_copy(
        mean, average, mean_send, mean_recv,
        device_id={"comp": 1 - comp}, device_id_type=MESH,
    )

    @pl.when(comp == 0)
    def _():
        depth = rows // 2
        turns = SUBCYCLES // depth
        clear_edges(turns)
        loads[0].wait()
        enter()
        pairs = [exchange_of(0, initial)]
        start(pairs[0])
        for copy in loads[1:]:
            copy.wait()
        covered = cover[...].astype(jnp.float32)
        push = covered / (inertia * forcing[0] + 1.0)
        own_stat[0] = forcing[1] * covered * (1.0 / 3.0)
        own_stat[1] = push
        own_stat[2] = push * (forcing[2] + current[0])
        own_stat[3] = push * (forcing[3] + current[1])
        stat_pair = stats_of(own_stat, 4)
        start(stat_pair)
        for turn in range(turns):
            source = initial if turn == 0 else own.at[turn - 1]
            if turn > 0:
                pairs.append(exchange_of(turn, source))
                start(pairs[turn])
            relay(pairs[turn])
            if turn == 0:
                relay(stat_pair)
                pl.semaphore_signal(
                    go, inc=1, device_id={"comp": 1 - comp}, device_id_type=MESH
                )
            fill_own(source)
            arrive(pairs[turn])
            if turn == 0:
                arrive(stat_pair)
                for place, block in enumerate((halo_stat.at[0], own_stat, halo_stat.at[1])):
                    span = slice(place * rows, (place + 1) * rows)
                    push = block[1]
                    stat[0, span] = block[0]
                    stat[1, span] = jnp.where(push > 0.0, 1.0 - push, 0.0)
                    stat[2, span] = 0.25 * push
                    stat[3, span] = block[2]
                    stat[4, span] = block[3]
            fill_sides(turn)

            def subcycle(step, carry):
                for chunk in range(chunks):
                    stress_stage(work, stat, chunk * width, width)
                for chunk in range(chunks):
                    velocity_stage(work, stat, total, chunk * width, width, rows)
                return carry

            lax.fori_loop(0, depth, subcycle, 0)
            final = state if turn == turns - 1 else own.at[turn]
            for field in range(fields):
                final[field] = work[field, rows : 2 * rows, inside]
        share = 1.0 / SUBCYCLES
        covered = cover[...].astype(jnp.float32)
        mean[0] = total[0] * share - covered * current[0]
        mean[1] = total[1] * share - covered * current[1]
        mean[2] = forcing[4] * covered * (total[2] * share)
        mean_copy.start()
        average[...] = mean[...]
        sent(stat_pair)
        for pair in pairs:
            sent(pair)
        mean_copy.wait_send()

    @pl.when(comp == 1)
    def _():
        depth = rows
        turns = SUBCYCLES // depth
        clear_edges(turns)
        spare[...] = jnp.zeros_like(spare)
        for copy in loads:
            copy.wait()
        enter()
        pl.semaphore_wait(go, 1)
        pairs = [exchange_of(0, initial)]
        start(pairs[0])
        stat_pair = stats_of(current, 2)
        start(stat_pair)
        for turn in range(turns):
            source = initial if turn == 0 else own.at[turn - 1]
            if turn > 0:
                pairs.append(exchange_of(turn, source))
                start(pairs[turn])
            relay(pairs[turn])
            if turn == 0:
                relay(stat_pair)
            fill_own(source)
            arrive(pairs[turn])
            if turn == 0:
                arrive(stat_pair)
                for place in range(3):
                    span = slice(place * rows, (place + 1) * rows)
                    for axis in range(2):
                        if place == 1:
                            speed = current[axis]
                        else:
                            speed = halo_stat[place // 2, axis]
                        stat[2 * axis, span] = courant * jnp.maximum(speed, 0.0)
                        stat[2 * axis + 1, span] = courant * jnp.minimum(speed, 0.0)
            fill_sides(turn)

            def substeps(step, carry):
                for chunk in range(chunks):
                    ocean_stage(work, spare, stat, chunk * width, width)
                for chunk in range(chunks):
                    ocean_stage(spare, work, stat, chunk * width, width)
                return carry

            lax.fori_loop(0, depth // 2, substeps, 0)
            final = state if turn == turns - 1 else own.at[turn]
            for field in range(fields):
                final[field] = work[field, rows : 2 * rows, inside]
        sent(stat_pair)
        for pair in pairs:
            sent(pair)
        mean_copy.wait_recv()


def run_turns(initial, forcing, current, cover):
    fields, rows, cols = initial.shape
    most = SUBCYCLES // (rows // 2)
    f32 = jnp.float32
    vmem = pl.BlockSpec(memory_space=pltpu.VMEM)
    dma = pltpu.SemaphoreType.DMA
    return pl.pallas_call(
        turns_kernel,
        out_shape=(
            jax.ShapeDtypeStruct((fields, rows, cols), f32),
            jax.ShapeDtypeStruct((3, rows, cols), f32),
        ),
        in_specs=[pl.BlockSpec(memory_space=pl.ANY)] * 4,
        out_specs=(vmem, vmem),
        scratch_shapes=[
            pltpu.VMEM(initial.shape, f32),
            pltpu.VMEM(forcing.shape, f32),
            pltpu.VMEM(current.shape, f32),
            pltpu.VMEM(cover.shape, cover.dtype),
            pltpu.VMEM((most, fields, rows, cols), f32),
            pltpu.VMEM((4, rows, cols), f32),
            pltpu.VMEM((most, 2, fields, rows, cols), f32),
            pltpu.VMEM((2, 4, rows, cols), f32),
            pltpu.VMEM((fields, 3 * rows, cols + 2 * PAD), f32),
            pltpu.VMEM((fields, 3 * rows, cols + 2 * PAD), f32),
            pltpu.VMEM((5, 3 * rows, cols), f32),
            pltpu.VMEM((3, rows, cols), f32),
            pltpu.VMEM((3, rows, cols), f32),
            dma((4,)),
            *[dma((most, fields * PARTS)) for _ in range(4)],
            *[dma((4 * PARTS,)) for _ in range(4)],
            dma, dma, pltpu.SemaphoreType.REGULAR,
        ],
        compiler_params=pltpu.CompilerParams(
            collective_id=0, has_side_effects=True
        ),
        name="turns",
    )(initial, forcing, current, cover)


def remap_kernel(average, targets, weights, window, acc, low_index, high_index):
    comp = lax.axis_index("comp")
    channels, rows, cols = average.shape
    span = low_index.shape[1]
    low_count, high_count = low_index.shape[0], high_index.shape[0]
    bf16 = jnp.bfloat16
    blocks = cols // low_count
    low_index[...] = lax.broadcasted_iota(jnp.int32, low_index.shape, 0).astype(bf16)
    high_index[...] = lax.broadcasted_iota(jnp.int32, high_index.shape, 0).astype(bf16)
    acc[...] = jnp.zeros_like(acc)

    def one_row(row, carry):
        for piece in range(cols // span):
            place = pl.ds(piece * span, span)
            target = targets[comp, pl.ds(row, 1), place]
            scale = weights[comp, pl.ds(row, 1), place].astype(jnp.float32) * (1.0 / weight_norm)
            low = lax.rem(target, low_count)
            block = lax.rem(lax.div(target, low_count), blocks)
            line = lax.div(target, cols)
            high = (lax.div(line, rows) * blocks + block) * rows + lax.rem(line, rows)
            low_hot = jnp.where(low_index[...] == low.astype(bf16), bf16(1), bf16(0))
            match = high_index[...] == high.astype(bf16)
            parts = []
            for channel in range(channels):
                value = average[channel, pl.ds(row, 1), place] * scale
                coarse = value.astype(bf16)
                fine = (value - coarse.astype(jnp.float32)).astype(bf16)
                parts.append(jnp.where(match, coarse, bf16(0)))
                parts.append(jnp.where(match, fine, bf16(0)))
            spread = jnp.concatenate(parts, axis=0)
            acc[...] += lax.dot_general(
                spread, low_hot, (((1,), (1,)), ((), ())), preferred_element_type=jnp.float32
            )
        return carry

    lax.fori_loop(0, rows, one_row, 0)
    for channel in range(channels):
        for half in range(2):
            for block in range(blocks):
                base = 2 * channel * high_count + (half * blocks + block) * rows
                window[channel, half, :, block * low_count : (block + 1) * low_count] = (
                    acc[base : base + rows] + acc[base + high_count : base + high_count + rows]
                )


def run_remap(average, targets, weights):
    channels, rows, cols = average.shape
    low_count = 256 if cols % 256 == 0 else 128
    high_count = 2 * rows * cols // low_count
    span = min(1024, cols)
    vmem = pl.BlockSpec(memory_space=pltpu.VMEM)
    return pl.pallas_call(
        remap_kernel,
        out_shape=jax.ShapeDtypeStruct((channels, 2, rows, cols), jnp.float32),
        in_specs=[vmem] * 3,
        out_specs=vmem,
        scratch_shapes=[
            pltpu.VMEM((2 * channels * high_count, low_count), jnp.float32),
            pltpu.VMEM((low_count, span), jnp.bfloat16),
            pltpu.VMEM((high_count, span), jnp.bfloat16),
        ],
        compiler_params=pltpu.CompilerParams(vmem_limit_bytes=40 * 1024 * 1024),
        name="remap",
    )(average, targets, weights)


def join_kernel(
    window, state, average, out_state, out_pair, beside, carry, before,
    side_send, side_recv, next_send, next_recv,
):
    me = lax.axis_index("blk")
    comp = lax.axis_index("comp")
    count = lax.axis_size("blk")
    right, left = lax.rem(me + 1, count), lax.rem(me + count - 1, count)
    barrier = pltpu.get_barrier_semaphore()
    pl.semaphore_signal(barrier, inc=1, device_id={"blk": right}, device_id_type=MESH)
    pl.semaphore_signal(barrier, inc=1, device_id={"blk": left}, device_id_type=MESH)
    pl.semaphore_signal(barrier, inc=1, device_id={"comp": 1 - comp}, device_id_type=MESH)
    pl.semaphore_wait(barrier, 3)
    channels = window.shape[0]
    sides, onward = [], []
    for half in (1, 0):
        for channel in range(channels):
            sides.append(
                pltpu.make_async_remote_copy(
                    window.at[channel, half], beside.at[channel, half],
                    side_send.at[half, channel], side_recv.at[half, channel],
                    device_id={"comp": 1 - comp}, device_id_type=MESH,
                )
            )
    for channel in range(channels):
        onward.append(
            pltpu.make_async_remote_copy(
                carry.at[channel], before.at[channel],
                next_send.at[channel], next_recv.at[channel],
                device_id={"blk": right}, device_id_type=MESH,
            )
        )

    @pl.when(comp == 0)
    def _():
        for copy in sides:
            copy.start()
        out_state[...] = state[...]
        out_pair[...] = average[...]
        for copy in sides:
            copy.wait_send()

    @pl.when(comp == 1)
    def _():
        for channel in range(channels):
            sides[channel].wait_recv()
            carry[channel] = window[channel, 1] + beside[channel, 1]
            onward[channel].start()
        for channel in range(channels):
            sides[channels + channel].wait_recv()
            out_pair[channel] = window[channel, 0] + beside[channel, 0]
        out_state[...] = state[...]
        for channel in range(channels):
            onward[channel].wait_recv()
            out_pair[channel] += before[channel]
        out_state[0] -= dilution * out_pair[2]
        for channel in range(channels):
            onward[channel].wait_send()


def run_join(window, state, average):
    channels, rows, cols = average.shape
    vmem = pl.BlockSpec(memory_space=pltpu.VMEM)
    dma = pltpu.SemaphoreType.DMA
    return pl.pallas_call(
        join_kernel,
        out_shape=(
            jax.ShapeDtypeStruct(state.shape, jnp.float32),
            jax.ShapeDtypeStruct(average.shape, jnp.float32),
        ),
        in_specs=[vmem] * 3,
        out_specs=(vmem, vmem),
        scratch_shapes=[
            pltpu.VMEM(window.shape, jnp.float32),
            pltpu.VMEM(average.shape, jnp.float32),
            pltpu.VMEM(average.shape, jnp.float32),
            dma((2, channels)), dma((2, channels)), dma((channels,)), dma((channels,)),
        ],
        compiler_params=pltpu.CompilerParams(
            collective_id=1, has_side_effects=True, vmem_limit_bytes=40 * 1024 * 1024
        ),
        name="join",
    )(window, state, average)


def body(initial, ice_forcing, ocean_current, ice_cover, targets, weights):
    state, average = run_turns(initial[0], ice_forcing, ocean_current, ice_cover)
    window = run_remap(average, targets, weights)
    state, coupled = run_join(window, state, average)
    return (state[None], coupled[None])


def solution(mesh):
    placed = (
        P("comp", None, "blk", None),
        P(None, "blk", None),
        P(None, "blk", None),
        P("blk", None),
        P(None, "blk", None),
        P(None, "blk", None),
    )
    return jax.shard_map(
        body,
        mesh=mesh,
        in_specs=placed,
        out_specs=(P("comp", None, "blk", None), P("comp", None, "blk", None)),
        check_vma=False,
    )
```

profile of v0, /device:TPU:1, one launch (start us, length us, event | category | flops | bytes accessed | tf_op | source)
XLA Modules:
  0.0 79.0 jit_solution(16105007502609251574)
XLA Ops:
  0.6 0.0 copy-start.3
  0.6 0.0 copy-start.4
  0.7 54.6 %turns.1 = (f32[5,8,2048]{2,1,0:T(8,128)}, f32[3,8,2048]{2,1,0:T(8,128)}) custom-call(f32[5,8,2048]{2,1,0:T(8,128)} %bitcast.5, f32[5,8,2048]{2,1,0:T(8,128)} %forcing_in.1, f32[2,8,2048]{2,1,0:T(8,128)} %current_in.1, s32[8,2048]{1,0:T(8,128)} %cover_in.1), custom_call_target="tpu_custom_call" | custom-call | tf_op jit(solution)/shard_map/turns/pallas_call | solution.py:356
  55.3 0.0 copy-done.3
  55.3 0.0 copy-done.4
  55.3 0.0 copy-start
  55.3 0.9 %copy-done = f32[3,8,2048]{2,1,0:T(8,128)S(1)} copy-done((f32[3,8,2048]{2,1,0:T(8,128)S(1)}, f32[3,8,2048]{2,1,0:T(8,128)}, u32[]{:S(2)}) %copy-start) | copy-done | bytes 196632
  56.2 0.0 copy-start.1
  56.2 0.0 copy-start.2
  56.2 8.4 %remap.1.window = f32[3,2,8,2048]{3,2,1,0:T(8,128)S(1)} custom-call(f32[3,8,2048]{2,1,0:T(8,128)S(1)} %copy-done, s32[2,8,2048]{2,1,0:T(8,128)S(1)} %copy-done.3, s32[2,8,2048]{2,1,0:T(8,128)S(1)} %copy-done.4), custom_call_target="tpu_custom_call" | custom-call | tf_op jit(solution)/shard_map/remap/pallas_call | solution.py:441
  64.7 0.0 copy-done.1
  64.7 0.0 copy-done.2
  64.7 12.9 %join.1 = (f32[5,8,2048]{2,1,0:T(8,128)S(1)}, f32[3,8,2048]{2,1,0:T(8,128)S(1)}) custom-call(f32[3,2,8,2048]{3,2,1,0:T(8,128)S(1)} %remap.1.window, f32[5,8,2048]{2,1,0:T(8,128)S(1)} %copy-done.2, f32[3,8,2048]{2,1,0:T(8,128)S(1)} %copy-done.1), custom_call_target="tpu_custom_call" | custom-call | tf_op jit(solution)/shard_map/join/pallas_call | solution.py:520
  77.6 0.7 copy.10
  78.3 0.7 copy.11
Async XLA Ops:
  0.6 54.7 %copy-start.3 = (s32[2,8,2048]{2,1,0:T(8,128)S(1)}, s32[2,8,2048]{2,1,0:T(8,128)}, u32[]{:S(2)}) copy-start(s32[2,8,2048]{2,1,0:T(8,128)} %targets.1) | copy-start | bytes 393220
  0.6 54.7 %copy-start.4 = (s32[2,8,2048]{2,1,0:T(8,128)S(1)}, s32[2,8,2048]{2,1,0:T(8,128)}, u32[]{:S(2)}) copy-start(s32[2,8,2048]{2,1,0:T(8,128)} %weights.1) | copy-start | bytes 393220
  55.3 0.9 %copy-start = (f32[3,8,2048]{2,1,0:T(8,128)S(1)}, f32[3,8,2048]{2,1,0:T(8,128)}, u32[]{:S(2)}) copy-start(f32[3,8,2048]{2,1,0:T(8,128)} %get-tuple-element.6.average) | copy-start | bytes 589828
  56.2 8.4 %copy-start.1 = (f32[3,8,2048]{2,1,0:T(8,128)S(1)}, f32[3,8,2048]{2,1,0:T(8,128)}, u32[]{:S(2)}) copy-start(f32[3,8,2048]{2,1,0:T(8,128)} %get-tuple-element.6.average) | copy-start | bytes 589828
  56.2 8.4 %copy-start.2 = (f32[5,8,2048]{2,1,0:T(8,128)S(1)}, f32[5,8,2048]{2,1,0:T(8,128)}, u32[]{:S(2)}) copy-start(f32[5,8,2048]{2,1,0:T(8,128)} %get-tuple-element.7.state) | copy-start | bytes 983044
where the time goes:
time: 79.1 us; the launch traced here: 79 us
  Pallas kernels  75.9 us (96%)
  local copies, waits for them, and re-layouts  2.34 us (3%)
    pallas_call x1, Pallas kernels, run_turns(): pl.pallas_call(turns_kernel, out_shape=(jax.ShapeDtypeStruct((fields, row...  54.6 us
    pallas_call x1, Pallas kernels, run_join(): pl.pallas_call(join_kernel, out_shape=(jax.ShapeDtypeStruct(state.shape,...  12.9 us
    pallas_call x1, Pallas kernels, run_remap(): pl.pallas_call(remap_kernel, out_shape=jax.ShapeDtypeStruct((channels, 2,...  8.41 us
    unnamed x12, local copies, waits for them, and re-layouts  2.34 us

commit v1 on v0

--- a/solution.py
+++ b/solution.py
@@ -387,6 +387,373 @@
     )(initial, forcing, current, cover)
 
 
+LANES = 128
+LEAD = 8
+ICE_REACH = 2 * SUBCYCLES
+SEA_REACH = SUBCYCLES
+
+
+def fits_tiles(count, rows, cols):
+    return count * rows == LANES and cols == count * LANES and count > 1
+
+
+def lane_index(shape):
+    return lax.broadcasted_iota(jnp.int32, shape, len(shape) - 1)
+
+
+def lane_diff(value):
+    lane = lane_index(value.shape)
+    after = jnp.where(lane == LANES - 1, 0.0, pltpu.roll(value, LANES - 1, 1))
+    before = jnp.where(lane == 0, 0.0, pltpu.roll(value, 1, 1))
+    return after - before
+
+
+def tile_stress(work, stat, low, size):
+    here, up, down = (pl.ds(low + shift, size) for shift in (0, 1, -1))
+    vel_x, vel_y = work[0, here], work[1, here]
+    cx = work[0, up] - work[0, down]
+    cy = work[1, up] - work[1, down]
+    rx, ry = lane_diff(vel_x), lane_diff(vel_y)
+    e_d = rx + cy
+    e_t = rx - cy
+    e_s = cx + ry
+    inv = lax.rsqrt(0.25 * (e_d * e_d) + 0.0625 * (e_t * e_t + e_s * e_s) + 0.01)
+    third = stat[0, here]
+    scaled = third * inv
+    one = 0.5 * scaled * e_d - third
+    two = 0.125 * scaled * e_t
+    work[2, here] = work[2, here] * (2.0 / 3.0) + (one + two)
+    work[3, here] = work[3, here] * (2.0 / 3.0) + (one - two)
+    work[4, here] = work[4, here] * (2.0 / 3.0) + 0.0625 * scaled * e_s
+
+
+def tile_velocity(work, stat, total, low, size, own):
+    here, up, down = (pl.ds(low + shift, size) for shift in (0, 1, -1))
+    force_x = lane_diff(work[2, here]) + 2.0 * (work[4, up] - work[4, down])
+    force_y = 2.0 * lane_diff(work[4, here]) + (work[3, up] - work[3, down])
+    old_x, old_y = work[0, here], work[1, here]
+    keep, push = stat[1, here], stat[2, here]
+    new_x = keep * (old_x + coriolis * old_y) + push * force_x + stat[3, here]
+    new_y = keep * (old_y - coriolis * old_x) + push * force_y + stat[4, here]
+    work[0, here] = new_x
+    work[1, here] = new_y
+    if own is not None:
+        place = pl.ds(own, size)
+        total[0, place] += new_x
+        total[1, place] += new_y
+        square = 1.0 + new_x * new_x + new_y * new_y
+        total[2, place] += square * lax.rsqrt(square)
+
+
+def tile_ocean(source, target, stat, low, size):
+    here, up, down = (pl.ds(low + shift, size) for shift in (0, 1, -1))
+    before, after, left, right, drain = (stat[i, here] for i in range(5))
+    for level, speed in enumerate(level_speed):
+        centre = source[level, here]
+        inflow = before * pltpu.roll(centre, 1, 1) + after * pltpu.roll(centre, LANES - 1, 1)
+        inflow += left * source[level, down] + right * source[level, up]
+        target[level, here] = centre + speed * (inflow - drain * centre)
+
+
+def pieces(low, high, step):
+    return [(start, min(step, high - start)) for start in range(low, high, step)]
+
+
+def tiles_kernel(
+    initial_in, forcing_in, current_in, cover_in, state, average,
+    pack, forcing, current, cover, recv, work, spare, stat, total, back, home, mean,
+    load, first_send, first_recv, second_send, second_recv,
+    total_send, total_recv, state_send, state_recv, mean_send, mean_recv, go,
+):
+    me = lax.axis_index("blk")
+    comp = lax.axis_index("comp")
+    count = lax.axis_size("blk")
+    fields, rows, cols = initial_in.shape
+    barrier = pltpu.get_barrier_semaphore()
+
+    def greet(where):
+        pl.semaphore_signal(barrier, inc=1, device_id=where, device_id_type=MESH)
+
+    def other(step):
+        return lax.rem(me + step, count)
+
+    steps = range(1, count)
+    for step in steps:
+        greet({"blk": other(step)})
+    greet({"comp": 1 - comp})
+
+    loads = [
+        pltpu.make_async_copy(source, target, load.at[i])
+        for i, (source, target) in enumerate(
+            (
+                (initial_in, pack.at[0:fields]),
+                (current_in, current),
+                (forcing_in, forcing),
+                (cover_in, cover),
+            )
+        )
+    ]
+    for copy in loads:
+        copy.start()
+
+    def lanes_of(block):
+        return pl.ds(pl.multiple_of(block * LANES, LANES), LANES)
+
+    def rows_of(block):
+        return pl.ds(pl.multiple_of(block * rows, rows), rows)
+
+    def outward(low, high, sems):
+        return [
+            pltpu.make_async_remote_copy(
+                pack.at[low:high, :, lanes_of(other(step))],
+                recv.at[low:high, rows_of(me), :],
+                sems[0].at[step], sems[1].at[step],
+                device_id={"blk": other(step)}, device_id_type=MESH,
+            )
+            for step in steps
+        ]
+
+    def homeward(source, target, sems):
+        return [
+            pltpu.make_async_remote_copy(
+                source.at[:, rows_of(other(step)), :],
+                target.at[:, :, lanes_of(me)],
+                sems[0].at[step], sems[1].at[step],
+                device_id={"blk": other(step)}, device_id_type=MESH,
+            )
+            for step in steps
+        ]
+
+    def start(copies):
+        for copy in copies:
+            copy.start()
+
+    def arrive(copies):
+        for copy in copies:
+            copy.wait_recv()
+
+    def sent(copies):
+        for copy in copies:
+            copy.wait_send()
+
+    def spread_edges(base, filled, reach):
+        group = LANES // (2 * reach)
+        lane = lane_index((rows, LANES))
+        slot = lane // (2 * reach)
+        leading = lane % (2 * reach) < reach
+        zero = jnp.zeros((rows, LANES), jnp.float32)
+        for tile in range(-(-filled // group)):
+            members = range(tile * group, min(filled, (tile + 1) * group))
+            turned = []
+            for block in range(count):
+                here = slice(block * LANES, (block + 1) * LANES)
+                merged = zero
+                for place, field in enumerate(members):
+                    shift = (2 * place + 1) * reach % LANES
+                    value = pack[field, :, here]
+                    moved = pltpu.roll(value, shift, 1) if shift else value
+                    merged = jnp.where(slot == place, moved, merged)
+                turned.append(merged)
+            for block in range(count):
+                before = turned[block - 1] if block > 0 else zero
+                after = turned[block + 1] if block < count - 1 else zero
+                here = slice(block * LANES, (block + 1) * LANES)
+                pack[base + tile, :, here] = jnp.where(leading, before, after)
+
+    def unpack(field, base, reach):
+        group = LANES // (2 * reach)
+        value = recv[field].T
+        edge = recv[base + field // group].T
+        low = field % group * 2 * reach
+        return jnp.concatenate(
+            [edge[low : low + reach], value, edge[low + reach : low + 2 * reach]], axis=0
+        )
+
+    mean_copy = pltpu.make_async_remote_copy(
+        mean, average, mean_send, mean_recv,
+        device_id={"comp": 1 - comp}, device_id_type=MESH,
+    )
+
+    @pl.when(comp == 0)
+    def _():
+        filled = fields + 4
+        packed = filled + -(-filled // (LANES // (2 * ICE_REACH)))
+        span = LANES + 2 * ICE_REACH
+        loads[0].wait()
+        pl.semaphore_wait(barrier, count)
+        first = outward(0, fields, (first_send, first_recv))
+        start(first)
+        for copy in loads[1:]:
+            copy.wait()
+        covered = cover[...].astype(jnp.float32)
+        push = covered / (inertia * forcing[0] + 1.0)
+        pack[fields] = forcing[1] * covered * (1.0 / 3.0)
+        pack[fields + 1] = push
+        pack[fields + 2] = push * (forcing[2] + current[0])
+        pack[fields + 3] = push * (forcing[3] + current[1])
+        spread_edges(filled, filled, ICE_REACH)
+        second = outward(fields, packed, (second_send, second_recv))
+        start(second)
+        recv[0:packed, rows_of(me), :] = pack[0:packed, :, lanes_of(me)]
+        total[...] = jnp.zeros_like(total)
+        for array in (work, stat):
+            for edge in (0, LEAD + span):
+                array[:, edge : edge + LEAD] = jnp.zeros((array.shape[0], LEAD, LANES), jnp.float32)
+        sent(first)
+        sent(second)
+        pl.semaphore_signal(go, inc=1, device_id={"comp": 1 - comp}, device_id_type=MESH)
+        arrive(first)
+        arrive(second)
+        whole = slice(LEAD, LEAD + span)
+        for field in range(2):
+            work[field, whole] = unpack(field, filled, ICE_REACH)
+        one, two = unpack(2, filled, ICE_REACH), unpack(3, filled, ICE_REACH)
+        work[2, whole] = one + two
+        work[3, whole] = one - two
+        work[4, whole] = unpack(4, filled, ICE_REACH)
+        stat[0, whole] = unpack(fields, filled, ICE_REACH)
+        push = unpack(fields + 1, filled, ICE_REACH)
+        stat[1, whole] = jnp.where(push > 0.0, 1.0 - push, 0.0)
+        stat[2, whole] = 0.25 * push
+        stat[3, whole] = unpack(fields + 2, filled, ICE_REACH)
+        stat[4, whole] = unpack(fields + 3, filled, ICE_REACH)
+
+        for group in range(SUBCYCLES // 4):
+            low, high = LEAD + 8 * group, LEAD + span - 8 * group
+            inner, outer = LEAD + ICE_REACH, LEAD + ICE_REACH + LANES
+
+            def subcycle(step, carry, low=low, high=high):
+                for begin, size in pieces(low, high, 16):
+                    tile_stress(work, stat, begin, size)
+                for begin, size in pieces(low, inner, 16) + pieces(outer, high, 16):
+                    tile_velocity(work, stat, total, begin, size, None)
+                for begin, size in pieces(inner, outer, 16):
+                    tile_velocity(work, stat, total, begin, size, begin - inner)
+                return carry
+
+            lax.fori_loop(0, 4, subcycle, 0)
+
+        own = slice(LEAD + ICE_REACH, LEAD + ICE_REACH + LANES)
+        for channel in range(3):
+            back[channel] = total[channel].T
+        totals = homeward(back.at[0:3], home, (total_send, total_recv))
+        start(totals)
+        one, two = work[2, own], work[3, own]
+        for field, value in enumerate(
+            (work[0, own], work[1, own], 0.5 * (one + two), 0.5 * (one - two), work[4, own])
+        ):
+            back[3 + field] = value.T
+        states = homeward(back.at[3 : 3 + fields], state, (state_send, state_recv))
+        start(states)
+        home[:, :, lanes_of(me)] = back[0:3, rows_of(me), :]
+        state[:, :, lanes_of(me)] = back[3 : 3 + fields, rows_of(me), :]
+        share = 1.0 / SUBCYCLES
+        covered = cover[...].astype(jnp.float32)
+        arrive(totals)
+        mean[0] = home[0] * share - covered * current[0]
+        mean[1] = home[1] * share - covered * current[1]
+        mean[2] = forcing[4] * covered * (home[2] * share)
+        mean_copy.start()
+        average[...] = mean[...]
+        sent(totals)
+        arrive(states)
+        sent(states)
+        mean_copy.wait_send()
+
+    @pl.when(comp == 1)
+    def _():
+        filled = fields + 2
+        packed = filled + -(-filled // (LANES // (2 * SEA_REACH)))
+        span = LANES + 2 * SEA_REACH
+        for copy in loads:
+            copy.wait()
+        for axis in range(2):
+            pack[fields + axis] = current[axis]
+        spread_edges(filled, filled, SEA_REACH)
+        for array in (work, spare):
+            for edge in (0, LEAD + span):
+                array[:, edge : edge + LEAD] = jnp.zeros((array.shape[0], LEAD, LANES), jnp.float32)
+        recv[0:packed, rows_of(me), :] = pack[0:packed, :, lanes_of(me)]
+        pl.semaphore_wait(barrier, count)
+        pl.semaphore_wait(go, 1)
+        first = outward(0, packed, (first_send, first_recv))
+        start(first)
+        arrive(first)
+        whole = slice(LEAD, LEAD + span)
+        for field in range(fields):
+            work[field, whole] = unpack(field, filled, SEA_REACH)
+        lane = lane_index((span, LANES))
+        speed = courant * unpack(fields, filled, SEA_REACH)
+        drain = jnp.abs(speed)
+        stat[0, whole] = jnp.where(lane == 0, 0.0, jnp.maximum(speed, 0.0))
+        stat[1, whole] = jnp.where(lane == LANES - 1, 0.0, -jnp.minimum(speed, 0.0))
+        speed = courant * unpack(fields + 1, filled, SEA_REACH)
+        stat[2, whole] = jnp.maximum(speed, 0.0)
+        stat[3, whole] = -jnp.minimum(speed, 0.0)
+        stat[4, whole] = drain + jnp.abs(speed)
+        for group in range(SUBCYCLES // 8):
+            low, high = LEAD + 8 * group, LEAD + span - 8 * group
+
+            def substeps(step, carry, low=low, high=high):
+                for begin, size in pieces(low, high, 16):
+                    tile_ocean(work, spare, stat, begin, size)
+                for begin, size in pieces(low, high, 16):
+                    tile_ocean(spare, work, stat, begin, size)
+                return carry
+
+            lax.fori_loop(0, 4, substeps, 0)
+        own = slice(LEAD + SEA_REACH, LEAD + SEA_REACH + LANES)
+        for field in range(fields):
+            back[3 + field] = work[field, own].T
+        states = homeward(back.at[3 : 3 + fields], state, (state_send, state_recv))
+        start(states)
+        state[:, :, lanes_of(me)] = back[3 : 3 + fields, rows_of(me), :]
+        sent(first)
+        mean_copy.wait_recv()
+        arrive(states)
+        sent(states)
+
+
+def run_tiles(initial, forcing, current, cover, count):
+    fields, rows, cols = initial.shape
+    f32 = jnp.float32
+    most = fields + 4
+    packed = most + -(-most // (LANES // (2 * ICE_REACH)))
+    tall = LANES + 2 * ICE_REACH + 2 * LEAD
+    vmem = pl.BlockSpec(memory_space=pltpu.VMEM)
+    dma = pltpu.SemaphoreType.DMA
+    return pl.pallas_call(
+        tiles_kernel,
+        out_shape=(
+            jax.ShapeDtypeStruct((fields, rows, cols), f32),
+            jax.ShapeDtypeStruct((3, rows, cols), f32),
+        ),
+        in_specs=[pl.BlockSpec(memory_space=pl.ANY)] * 4,
+        out_specs=(vmem, vmem),
+        scratch_shapes=[
+            pltpu.VMEM((packed, rows, cols), f32),
+            pltpu.VMEM(forcing.shape, f32),
+            pltpu.VMEM(current.shape, f32),
+            pltpu.VMEM(cover.shape, cover.dtype),
+            pltpu.VMEM((packed, LANES, LANES), f32),
+            pltpu.VMEM((fields, tall, LANES), f32),
+            pltpu.VMEM((fields, tall, LANES), f32),
+            pltpu.VMEM((5, tall, LANES), f32),
+            pltpu.VMEM((3, LANES, LANES), f32),
+            pltpu.VMEM((3 + fields, LANES, LANES), f32),
+            pltpu.VMEM((3, rows, cols), f32),
+            pltpu.VMEM((3, rows, cols), f32),
+            dma((4,)),
+            *[dma((count,)) for _ in range(8)],
+            dma, dma, pltpu.SemaphoreType.REGULAR,
+        ],
+        compiler_params=pltpu.CompilerParams(
+            collective_id=0, has_side_effects=True, vmem_limit_bytes=40 * 1024 * 1024
+        ),
+        name="tiles",
+    )(initial, forcing, current, cover)
+
+
 def remap_kernel(average, targets, weights, window, acc, low_index, high_index):
     comp = lax.axis_index("comp")
     channels, rows, cols = average.shape
@@ -538,8 +905,11 @@
     )(window, state, average)
 
 
-def body(initial, ice_forcing, ocean_current, ice_cover, targets, weights):
-    state, average = run_turns(initial[0], ice_forcing, ocean_current, ice_cover)
+def body(count, initial, ice_forcing, ocean_current, ice_cover, targets, weights):
+    if fits_tiles(count, *initial.shape[2:]):
+        state, average = run_tiles(initial[0], ice_forcing, ocean_current, ice_cover, count)
+    else:
+        state, average = run_turns(initial[0], ice_forcing, ocean_current, ice_cover)
     window = run_remap(average, targets, weights)
     state, coupled = run_join(window, state, average)
     return (state[None], coupled[None])
@@ -555,7 +925,7 @@
         P(None, "blk", None),
     )
     return jax.shard_map(
-        body,
+        functools.partial(body, mesh.shape["blk"]),
         mesh=mesh,
         in_specs=placed,
         out_specs=(P("comp", None, "blk", None), P("comp", None, "blk", None)),

time: 79.1 us -> 61.2 us (0.77)
  Pallas kernels: 75.9 us -> 55.2 us
  local copies, waits for them, and re-layouts: 2.34 us -> 5.09 us
    pallas_call x1, Pallas kernels: 54.6 us -> 37.3 us  [run_tiles(): pl.pallas_call(tiles_kernel, out_shape=(jax.ShapeDtypeStruct((fields, row...]
    pallas_call x1, Pallas kernels: 12.9 us -> 9.41 us  [run_join(): pl.pallas_call(join_kernel, out_shape=(jax.ShapeDtypeStruct(state.shape,...]
    unnamed x12 -> x14, local copies, waits for them, and re-layouts: 2.34 us -> 5.09 us
where the time goes in v1:
time: 61.2 us; the launch traced here: 60.9 us
  Pallas kernels  55.2 us (90%)
  local copies, waits for them, and re-layouts  5.09 us (8%)
  between operations  0.68 us (1%)
    pallas_call x1, Pallas kernels, run_tiles(): pl.pallas_call(tiles_kernel, out_shape=(jax.ShapeDtypeStruct((fields, row...  37.3 us
    pallas_call x1, Pallas kernels, run_join(): pl.pallas_call(join_kernel, out_shape=(jax.ShapeDtypeStruct(state.shape,...  9.41 us
    pallas_call x1, Pallas kernels, run_remap(): pl.pallas_call(remap_kernel, out_shape=jax.ShapeDtypeStruct((channels, 2,...  8.41 us
    unnamed x14, local copies, waits for them, and re-layouts  5.09 us

profile of v1, /device:TPU:1, one launch (start us, length us, event | category | flops | bytes accessed | tf_op | source)
XLA Modules:
  0.0 60.9 jit_solution(4287183146833991309)
XLA Ops:
  0.6 0.0 copy-start
  0.6 1.0 %copy-done = f32[1,5,8,2048]{3,2,1,0:T(8,128)S(1)} copy-done((f32[1,5,8,2048]{3,2,1,0:T(8,128)S(1)}, f32[1,5,8,2048]{3,2,1,0:T(8,128)}, u32[]{:S(2)}) %copy-start) | copy-done | bytes 327704
  1.6 0.0 copy-start.1
  1.6 1.0 %copy-done.1 = f32[5,8,2048]{2,1,0:T(8,128)S(1)} copy-done((f32[5,8,2048]{2,1,0:T(8,128)S(1)}, f32[5,8,2048]{2,1,0:T(8,128)}, u32[]{:S(2)}) %copy-start.1) | copy-done | bytes 327704
  2.6 0.0 copy-start.2
  2.6 0.9 %copy-done.2 = f32[2,8,2048]{2,1,0:T(8,128)S(1)} copy-done((f32[2,8,2048]{2,1,0:T(8,128)S(1)}, f32[2,8,2048]{2,1,0:T(8,128)}, u32[]{:S(2)}) %copy-start.2) | copy-done | bytes 131096
  3.5 0.0 copy-start.5
  3.5 0.8 %copy-done.5 = s32[8,2048]{1,0:T(8,128)S(1)} copy-done((s32[8,2048]{1,0:T(8,128)S(1)}, s32[8,2048]{1,0:T(8,128)}, u32[]{:S(2)}) %copy-start.5) | copy-done | bytes 65560
  4.3 0.0 copy-start.3
  4.3 0.0 copy-start.4
  4.3 37.3 %tiles.1 = (f32[5,8,2048]{2,1,0:T(8,128)S(1)}, f32[3,8,2048]{2,1,0:T(8,128)S(1)}) custom-call(f32[5,8,2048]{2,1,0:T(8,128)S(1)} %bitcast.3, f32[5,8,2048]{2,1,0:T(8,128)S(1)} %copy-done.1, f32[2,8,2048]{2,1,0:T(8,128)S(1)} %copy-done.2, s32[8,2048]{1,0:T(8,128)S(1)} %copy-done.5), custom_call_target="tpu_custom_call" | custom-call | tf_op jit(solution)/shard_map/tiles/pallas_call | solution.py:725
  41.7 0.0 copy-done.3
  41.7 0.0 copy-done.4
  41.7 8.4 %remap.1.window = f32[3,2,8,2048]{3,2,1,0:T(8,128)S(1)} custom-call(f32[3,8,2048]{2,1,0:T(8,128)S(1)} %get-tuple-element.6.average, s32[2,8,2048]{2,1,0:T(8,128)S(1)} %copy-done.3, s32[2,8,2048]{2,1,0:T(8,128)S(1)} %copy-done.4), custom_call_target="tpu_custom_call" | custom-call | tf_op jit(solution)/shard_map/remap/pallas_call | solution.py:808
  50.1 9.4 %join.1 = (f32[5,8,2048]{2,1,0:T(8,128)S(1)}, f32[3,8,2048]{2,1,0:T(8,128)S(1)}) custom-call(f32[3,2,8,2048]{3,2,1,0:T(8,128)S(1)} %remap.1.window, f32[5,8,2048]{2,1,0:T(8,128)S(1)} %get-tuple-element.7.state, f32[3,8,2048]{2,1,0:T(8,128)S(1)} %get-tuple-element.6.average), custom_call_target="tpu_custom_call" | custom-call | tf_op jit(solution)/shard_map/join/pallas_call | solution.py:887
  59.5 0.7 %copy.10 = f32[1,5,8,2048]{3,2,1,0:T(8,128)} copy(f32[1,5,8,2048]{3,2,1,0:T(8,128)S(1)} %bitcast.4) | data formatting | bytes 655360
  60.3 0.7 %copy.11 = f32[1,3,8,2048]{3,2,1,0:T(8,128)} copy(f32[1,3,8,2048]{3,2,1,0:T(8,128)S(1)} %bitcast.5) | data formatting | bytes 393216
Async XLA Ops:
  0.6 1.0 %copy-start = (f32[1,5,8,2048]{3,2,1,0:T(8,128)S(1)}, f32[1,5,8,2048]{3,2,1,0:T(8,128)}, u32[]{:S(2)}) copy-start(f32[1,5,8,2048]{3,2,1,0:T(8,128)} %param.6) | copy-start | bytes 983044
  1.6 1.0 %copy-start.1 = (f32[5,8,2048]{2,1,0:T(8,128)S(1)}, f32[5,8,2048]{2,1,0:T(8,128)}, u32[]{:S(2)}) copy-start(f32[5,8,2048]{2,1,0:T(8,128)} %forcing_in.1) | copy-start | bytes 983044
  2.6 0.9 %copy-start.2 = (f32[2,8,2048]{2,1,0:T(8,128)S(1)}, f32[2,8,2048]{2,1,0:T(8,128)}, u32[]{:S(2)}) copy-start(f32[2,8,2048]{2,1,0:T(8,128)} %current_in.1) | copy-start | bytes 393220
  3.5 0.8 %copy-start.5 = (s32[8,2048]{1,0:T(8,128)S(1)}, s32[8,2048]{1,0:T(8,128)}, u32[]{:S(2)}) copy-start(s32[8,2048]{1,0:T(8,128)} %cover_in.1) | copy-start | bytes 196612
  4.3 37.4 %copy-start.3 = (s32[2,8,2048]{2,1,0:T(8,128)S(1)}, s32[2,8,2048]{2,1,0:T(8,128)}, u32[]{:S(2)}) copy-start(s32[2,8,2048]{2,1,0:T(8,128)} %targets.1) | copy-start | bytes 393220
  4.3 37.4 %copy-start.4 = (s32[2,8,2048]{2,1,0:T(8,128)S(1)}, s32[2,8,2048]{2,1,0:T(8,128)}, u32[]{:S(2)}) copy-start(s32[2,8,2048]{2,1,0:T(8,128)} %weights.1) | copy-start | bytes 393220

commit v2 on v1

--- a/solution.py
+++ b/solution.py
@@ -460,10 +460,13 @@
 
 
 def tiles_kernel(
-    initial_in, forcing_in, current_in, cover_in, state, average,
-    pack, forcing, current, cover, recv, work, spare, stat, total, back, home, mean,
+    initial_in, forcing_in, current_in, cover_in, targets_in, weights_in, state, pair,
+    pack, forcing, current, cover, targets, weights,
+    recv, work, spare, stat, total, back, home, mean, acc, window, beside, before,
+    low_index, high_index,
     load, first_send, first_recv, second_send, second_recv,
-    total_send, total_recv, state_send, state_recv, mean_send, mean_recv, go,
+    total_send, total_recv, state_send, state_recv, mean_send, mean_recv,
+    side_send, side_recv, next_send, next_recv, go,
 ):
     me = lax.axis_index("blk")
     comp = lax.axis_index("comp")
@@ -490,6 +493,8 @@
                 (current_in, current),
                 (forcing_in, forcing),
                 (cover_in, cover),
+                (targets_in.at[comp], targets),
+                (weights_in.at[comp], weights),
             )
         )
     ]
@@ -569,10 +574,72 @@
             [edge[low : low + reach], value, edge[low + reach : low + 2 * reach]], axis=0
         )
 
+    channels = pair.shape[0]
     mean_copy = pltpu.make_async_remote_copy(
-        mean, average, mean_send, mean_recv,
+        mean, home, mean_send, mean_recv,
         device_id={"comp": 1 - comp}, device_id_type=MESH,
     )
+    sides = [
+        [
+            pltpu.make_async_remote_copy(
+                window.at[half, channel], beside.at[half, channel],
+                side_send.at[half, channel], side_recv.at[half, channel],
+                device_id={"comp": 1 - comp}, device_id_type=MESH,
+            )
+            for channel in range(channels)
+        ]
+        for half in range(2)
+    ]
+    onward = [
+        pltpu.make_async_remote_copy(
+            window.at[1, channel], before.at[channel],
+            next_send.at[channel], next_recv.at[channel],
+            device_id={"blk": other(1)}, device_id_type=MESH,
+        )
+        for channel in range(channels)
+    ]
+
+    def prepare_remap():
+        low_index[...] = lax.broadcasted_iota(jnp.int32, low_index.shape, 0).astype(low_index.dtype)
+        high_index[...] = lax.broadcasted_iota(jnp.int32, high_index.shape, 0).astype(high_index.dtype)
+
+    def remap(values, half):
+        low_count, high_count = low_index.shape[0], high_index.shape[0]
+        blocks = cols // low_count
+        bf16 = jnp.bfloat16
+        acc[...] = jnp.zeros_like(acc)
+
+        def one_row(row, carry):
+            place = pl.ds(row, 1)
+            target = targets[place, :]
+            scale = weights[place, :].astype(jnp.float32) * (1.0 / weight_norm)
+            low = lax.rem(target, low_count)
+            block = lax.rem(lax.div(target, low_count), blocks)
+            line = lax.div(target, cols) - half * rows
+            high = block * rows + line
+            high = jnp.where(jnp.logical_and(line >= 0, line < rows), high, high_count)
+            low_hot = jnp.where(low_index[...] == low.astype(bf16), bf16(1), bf16(0))
+            match = high_index[...] == high.astype(bf16)
+            parts = []
+            for channel in range(channels):
+                value = values[channel, place, :] * scale
+                coarse = value.astype(bf16)
+                fine = (value - coarse.astype(jnp.float32)).astype(bf16)
+                parts.append(jnp.where(match, coarse, bf16(0)))
+                parts.append(jnp.where(match, fine, bf16(0)))
+            spread = jnp.concatenate(parts, axis=0)
+            acc[...] += lax.dot_general(
+                spread, low_hot, (((1,), (1,)), ((), ())), preferred_element_type=jnp.float32
+            )
+            return carry
+
+        lax.fori_loop(0, rows, one_row, 0)
+        for channel in range(channels):
+            for block in range(blocks):
+                base = 2 * channel * high_count + block * rows
+                window[half, channel, :, block * low_count : (block + 1) * low_count] = (
+                    acc[base : base + rows] + acc[base + high_count : base + high_count + rows]
+                )
 
     @pl.when(comp == 0)
     def _():
@@ -583,7 +650,7 @@
         pl.semaphore_wait(barrier, count)
         first = outward(0, fields, (first_send, first_recv))
         start(first)
-        for copy in loads[1:]:
+        for copy in loads[1:4]:
             copy.wait()
         covered = cover[...].astype(jnp.float32)
         push = covered / (inertia * forcing[0] + 1.0)
@@ -599,6 +666,9 @@
         for array in (work, stat):
             for edge in (0, LEAD + span):
                 array[:, edge : edge + LEAD] = jnp.zeros((array.shape[0], LEAD, LANES), jnp.float32)
+        prepare_remap()
+        for copy in loads[4:]:
+            copy.wait()
         sent(first)
         sent(second)
         pl.semaphore_signal(go, inc=1, device_id={"comp": 1 - comp}, device_id_type=MESH)
@@ -654,11 +724,15 @@
         mean[1] = home[1] * share - covered * current[1]
         mean[2] = forcing[4] * covered * (home[2] * share)
         mean_copy.start()
-        average[...] = mean[...]
+        pair[...] = mean[...]
+        for half in (1, 0):
+            remap(mean, half)
+            start(sides[half])
         sent(totals)
         arrive(states)
         sent(states)
         mean_copy.wait_send()
+        sent(sides[0] + sides[1])
 
     @pl.when(comp == 1)
     def _():
@@ -674,6 +748,7 @@
             for edge in (0, LEAD + span):
                 array[:, edge : edge + LEAD] = jnp.zeros((array.shape[0], LEAD, LANES), jnp.float32)
         recv[0:packed, rows_of(me), :] = pack[0:packed, :, lanes_of(me)]
+        prepare_remap()
         pl.semaphore_wait(barrier, count)
         pl.semaphore_wait(go, 1)
         first = outward(0, packed, (first_send, first_recv))
@@ -710,16 +785,31 @@
         state[:, :, lanes_of(me)] = back[3 : 3 + fields, rows_of(me), :]
         sent(first)
         mean_copy.wait_recv()
+        remap(home, 1)
+        for channel in range(channels):
+            sides[1][channel].wait_recv()
+            window[1, channel] += beside[1, channel]
+            onward[channel].start()
+        remap(home, 0)
+        for channel in range(channels):
+            sides[0][channel].wait_recv()
+            pair[channel] = window[0, channel] + beside[0, channel]
         arrive(states)
+        arrive(onward)
+        pair[...] += before[...]
+        state[0] -= dilution * pair[2]
         sent(states)
-
-
-def run_tiles(initial, forcing, current, cover, count):
+        sent(onward)
+
+
+def run_tiles(initial, forcing, current, cover, targets, weights, count):
     fields, rows, cols = initial.shape
     f32 = jnp.float32
     most = fields + 4
     packed = most + -(-most // (LANES // (2 * ICE_REACH)))
     tall = LANES + 2 * ICE_REACH + 2 * LEAD
+    low_count = 256 if cols % 256 == 0 else 128
+    high_count = rows * cols // low_count
     vmem = pl.BlockSpec(memory_space=pltpu.VMEM)
     dma = pltpu.SemaphoreType.DMA
     return pl.pallas_call(
@@ -728,13 +818,15 @@
             jax.ShapeDtypeStruct((fields, rows, cols), f32),
             jax.ShapeDtypeStruct((3, rows, cols), f32),
         ),
-        in_specs=[pl.BlockSpec(memory_space=pl.ANY)] * 4,
+        in_specs=[pl.BlockSpec(memory_space=pl.ANY)] * 6,
         out_specs=(vmem, vmem),
         scratch_shapes=[
             pltpu.VMEM((packed, rows, cols), f32),
             pltpu.VMEM(forcing.shape, f32),
             pltpu.VMEM(current.shape, f32),
             pltpu.VMEM(cover.shape, cover.dtype),
+            pltpu.VMEM(targets.shape[1:], targets.dtype),
+            pltpu.VMEM(weights.shape[1:], weights.dtype),
             pltpu.VMEM((packed, LANES, LANES), f32),
             pltpu.VMEM((fields, tall, LANES), f32),
             pltpu.VMEM((fields, tall, LANES), f32),
@@ -743,15 +835,22 @@
             pltpu.VMEM((3 + fields, LANES, LANES), f32),
             pltpu.VMEM((3, rows, cols), f32),
             pltpu.VMEM((3, rows, cols), f32),
-            dma((4,)),
+            pltpu.VMEM((6 * high_count, low_count), f32),
+            pltpu.VMEM((2, 3, rows, cols), f32),
+            pltpu.VMEM((2, 3, rows, cols), f32),
+            pltpu.VMEM((3, rows, cols), f32),
+            pltpu.VMEM((low_count, cols), jnp.bfloat16),
+            pltpu.VMEM((high_count, cols), jnp.bfloat16),
+            dma((6,)),
             *[dma((count,)) for _ in range(8)],
-            dma, dma, pltpu.SemaphoreType.REGULAR,
+            dma, dma, dma((2, 3)), dma((2, 3)), dma((3,)), dma((3,)),
+            pltpu.SemaphoreType.REGULAR,
         ],
         compiler_params=pltpu.CompilerParams(
             collective_id=0, has_side_effects=True, vmem_limit_bytes=40 * 1024 * 1024
         ),
         name="tiles",
-    )(initial, forcing, current, cover)
+    )(initial, forcing, current, cover, targets, weights)
 
 
 def remap_kernel(average, targets, weights, window, acc, low_index, high_index):
@@ -907,11 +1006,13 @@
 
 def body(count, initial, ice_forcing, ocean_current, ice_cover, targets, weights):
     if fits_tiles(count, *initial.shape[2:]):
-        state, average = run_tiles(initial[0], ice_forcing, ocean_current, ice_cover, count)
+        state, coupled = run_tiles(
+            initial[0], ice_forcing, ocean_current, ice_cover, targets, weights, count
+        )
     else:
         state, average = run_turns(initial[0], ice_forcing, ocean_current, ice_cover)
-    window = run_remap(average, targets, weights)
-    state, coupled = run_join(window, state, average)
+        window = run_remap(average, targets, weights)
+        state, coupled = run_join(window, state, average)
     return (state[None], coupled[None])
 
 

time: 61.2 us -> 54 us (0.88)
  Pallas kernels: 55.2 us -> 46.2 us
  local copies, waits for them, and re-layouts: 5.09 us -> 6.89 us
    pallas_call x2 -> x0, Pallas kernels: 17.8 us -> none  [the longest x1 9.41 us: run_join(): pl.pallas_call(join_kernel, out_shape=(jax.ShapeDtypeStruct(state.shape,...]
    pallas_call x1, Pallas kernels: 37.3 us -> 46.2 us  [run_tiles(): pl.pallas_call(tiles_kernel, out_shape=(jax.ShapeDtypeStruct((fields, row...]
    unnamed x14, local copies, waits for them, and re-layouts: 5.09 us -> 6.89 us
where the time goes in v2:
time: 54 us; the launch traced here: 53.7 us
  Pallas kernels  46.2 us (86%)
  local copies, waits for them, and re-layouts  6.89 us (13%)
  between operations  0.65 us (1%)
    pallas_call x1, Pallas kernels, run_tiles(): pl.pallas_call(tiles_kernel, out_shape=(jax.ShapeDtypeStruct((fields, row...  46.2 us
    unnamed x14, local copies, waits for them, and re-layouts  6.89 us

profile of v2, /device:TPU:1, one launch (start us, length us, event | category | flops | bytes accessed | tf_op | source)
XLA Modules:
  0.0 53.7 jit_solution(13908629438324530623)
XLA Ops:
  0.6 0.0 copy-start
  0.6 1.0 %copy-done = f32[1,5,8,2048]{3,2,1,0:T(8,128)S(1)} copy-done((f32[1,5,8,2048]{3,2,1,0:T(8,128)S(1)}, f32[1,5,8,2048]{3,2,1,0:T(8,128)}, u32[]{:S(2)}) %copy-start) | copy-done | bytes 327704
  1.6 0.0 copy-start.1
  1.6 1.0 %copy-done.1 = f32[5,8,2048]{2,1,0:T(8,128)S(1)} copy-done((f32[5,8,2048]{2,1,0:T(8,128)S(1)}, f32[5,8,2048]{2,1,0:T(8,128)}, u32[]{:S(2)}) %copy-start.1) | copy-done | bytes 327704
  2.6 0.0 copy-start.2
  2.6 0.9 %copy-done.2 = f32[2,8,2048]{2,1,0:T(8,128)S(1)} copy-done((f32[2,8,2048]{2,1,0:T(8,128)S(1)}, f32[2,8,2048]{2,1,0:T(8,128)}, u32[]{:S(2)}) %copy-start.2) | copy-done | bytes 131096
  3.5 0.0 copy-start.3
  3.5 0.9 %copy-done.3 = s32[2,8,2048]{2,1,0:T(8,128)S(1)} copy-done((s32[2,8,2048]{2,1,0:T(8,128)S(1)}, s32[2,8,2048]{2,1,0:T(8,128)}, u32[]{:S(2)}) %copy-start.3) | copy-done | bytes 131096
  4.4 0.0 copy-start.4
  4.4 0.9 %copy-done.4 = s32[2,8,2048]{2,1,0:T(8,128)S(1)} copy-done((s32[2,8,2048]{2,1,0:T(8,128)S(1)}, s32[2,8,2048]{2,1,0:T(8,128)}, u32[]{:S(2)}) %copy-start.4) | copy-done | bytes 131096
  5.3 0.0 copy-start.5
  5.3 0.8 %copy-done.5 = s32[8,2048]{1,0:T(8,128)S(1)} copy-done((s32[8,2048]{1,0:T(8,128)S(1)}, s32[8,2048]{1,0:T(8,128)}, u32[]{:S(2)}) %copy-start.5) | copy-done | bytes 65560
  6.1 46.2 %tiles.1 = (f32[5,8,2048]{2,1,0:T(8,128)S(1)}, f32[3,8,2048]{2,1,0:T(8,128)S(1)}) custom-call(f32[5,8,2048]{2,1,0:T(8,128)S(1)} %bitcast.4, f32[5,8,2048]{2,1,0:T(8,128)S(1)} %copy-done.1, f32[2,8,2048]{2,1,0:T(8,128)S(1)} %copy-done.2, s32[8,2048]{1,0:T(8,128)S(1)} %copy-done.5, s32[2,8,2048]{2,1,0:T(8,128)S(1)} %copy-done.3, s32[2,8,2048]{2,1,0:T(8,128)S(1)} %copy-done.4), custom_call_target="tpu_custom_call" | custom-call | tf_op jit(solution)/shard_map/tiles/pallas_call | solution.py:815
  52.3 0.7 %copy.10 = f32[1,5,8,2048]{3,2,1,0:T(8,128)} copy(f32[1,5,8,2048]{3,2,1,0:T(8,128)S(1)} %bitcast.3) | data formatting | bytes 655360
  53.0 0.7 %copy.11 = f32[1,3,8,2048]{3,2,1,0:T(8,128)} copy(f32[1,3,8,2048]{3,2,1,0:T(8,128)S(1)} %bitcast.5) | data formatting | bytes 393216
Async XLA Ops:
  0.6 1.0 %copy-start = (f32[1,5,8,2048]{3,2,1,0:T(8,128)S(1)}, f32[1,5,8,2048]{3,2,1,0:T(8,128)}, u32[]{:S(2)}) copy-start(f32[1,5,8,2048]{3,2,1,0:T(8,128)} %param.6) | copy-start | bytes 983044
  1.6 1.0 %copy-start.1 = (f32[5,8,2048]{2,1,0:T(8,128)S(1)}, f32[5,8,2048]{2,1,0:T(8,128)}, u32[]{:S(2)}) copy-start(f32[5,8,2048]{2,1,0:T(8,128)} %forcing_in.1) | copy-start | bytes 983044
  2.6 0.9 %copy-start.2 = (f32[2,8,2048]{2,1,0:T(8,128)S(1)}, f32[2,8,2048]{2,1,0:T(8,128)}, u32[]{:S(2)}) copy-start(f32[2,8,2048]{2,1,0:T(8,128)} %current_in.1) | copy-start | bytes 393220
  3.5 0.9 %copy-start.3 = (s32[2,8,2048]{2,1,0:T(8,128)S(1)}, s32[2,8,2048]{2,1,0:T(8,128)}, u32[]{:S(2)}) copy-start(s32[2,8,2048]{2,1,0:T(8,128)} %targets_in.1) | copy-start | bytes 393220
  4.4 0.9 %copy-start.4 = (s32[2,8,2048]{2,1,0:T(8,128)S(1)}, s32[2,8,2048]{2,1,0:T(8,128)}, u32[]{:S(2)}) copy-start(s32[2,8,2048]{2,1,0:T(8,128)} %weights_in.1) | copy-start | bytes 393220
  5.3 0.8 %copy-start.5 = (s32[8,2048]{1,0:T(8,128)S(1)}, s32[8,2048]{1,0:T(8,128)}, u32[]{:S(2)}) copy-start(s32[8,2048]{1,0:T(8,128)} %cover_in.1) | copy-start | bytes 196612

commit v3 on v2

--- a/solution.py
+++ b/solution.py
@@ -463,7 +463,7 @@
     initial_in, forcing_in, current_in, cover_in, targets_in, weights_in, state, pair,
     pack, forcing, current, cover, targets, weights,
     recv, work, spare, stat, total, back, home, mean, acc, window, beside, before,
-    low_index, high_index,
+    low, high, hot, parts,
     load, first_send, first_recv, second_send, second_recv,
     total_send, total_recv, state_send, state_recv, mean_send, mean_recv,
     side_send, side_recv, next_send, next_recv, go,
@@ -600,36 +600,58 @@
     ]
 
     def prepare_remap():
-        low_index[...] = lax.broadcasted_iota(jnp.int32, low_index.shape, 0).astype(low_index.dtype)
-        high_index[...] = lax.broadcasted_iota(jnp.int32, high_index.shape, 0).astype(high_index.dtype)
-
-    def remap(values, half):
-        low_count, high_count = low_index.shape[0], high_index.shape[0]
+        low_count = hot.shape[1]
         blocks = cols // low_count
+        target = targets[...]
+        block = lax.rem(lax.div(target, low_count), blocks)
+        line = lax.div(target, cols)
+        low[...] = lax.rem(target, low_count).astype(jnp.float32)
+        for half in range(2):
+            inside = lax.div(line, rows) == half
+            place = block * rows + line - half * rows
+            high[half] = jnp.where(inside, place, blocks * rows).astype(jnp.float32)
+
+        def one_row(row, carry):
+            lane = lane_index((LANES, LANES)).astype(jnp.float32)
+            line = low[pl.ds(row, 1), :]
+            for start in range(0, cols, LANES):
+                value = jnp.broadcast_to(line[:, start : start + LANES], (LANES, LANES)).T
+                place = pl.ds(pl.multiple_of(row * cols + start, LANES), LANES)
+                for first in range(0, low_count, LANES):
+                    hit = jnp.where(value == lane + float(first), 1.0, 0.0)
+                    hot[place, first : first + LANES] = hit.astype(hot.dtype)
+            return carry
+
+        lax.fori_loop(0, rows, one_row, 0)
+
+    def split_values(values):
+        scale = weights[...].astype(jnp.float32) * (1.0 / weight_norm)
+        for channel in range(channels):
+            value = values[channel] * scale
+            coarse = value.astype(jnp.bfloat16).astype(jnp.float32)
+            parts[2 * channel] = coarse
+            parts[2 * channel + 1] = value - coarse
+
+    def remap(half):
+        low_count = hot.shape[1]
+        blocks = cols // low_count
+        high_count = blocks * rows
         bf16 = jnp.bfloat16
+        tall = 16
         acc[...] = jnp.zeros_like(acc)
 
         def one_row(row, carry):
             place = pl.ds(row, 1)
-            target = targets[place, :]
-            scale = weights[place, :].astype(jnp.float32) * (1.0 / weight_norm)
-            low = lax.rem(target, low_count)
-            block = lax.rem(lax.div(target, low_count), blocks)
-            line = lax.div(target, cols) - half * rows
-            high = block * rows + line
-            high = jnp.where(jnp.logical_and(line >= 0, line < rows), high, high_count)
-            low_hot = jnp.where(low_index[...] == low.astype(bf16), bf16(1), bf16(0))
-            match = high_index[...] == high.astype(bf16)
-            parts = []
-            for channel in range(channels):
-                value = values[channel, place, :] * scale
-                coarse = value.astype(bf16)
-                fine = (value - coarse.astype(jnp.float32)).astype(bf16)
-                parts.append(jnp.where(match, coarse, bf16(0)))
-                parts.append(jnp.where(match, fine, bf16(0)))
-            spread = jnp.concatenate(parts, axis=0)
-            acc[...] += lax.dot_general(
-                spread, low_hot, (((1,), (1,)), ((), ())), preferred_element_type=jnp.float32
+            level = jnp.broadcast_to(high[half, place, :], (tall, cols)).astype(bf16)
+            index = lax.broadcasted_iota(jnp.int32, (tall, cols), 0).astype(bf16)
+            matches = [level == index + bf16(first) for first in range(0, high_count, tall)]
+            spread = []
+            for part in range(2 * channels):
+                value = jnp.broadcast_to(parts[part, place, :], (tall, cols)).astype(bf16)
+                spread += [jnp.where(match, value, bf16(0)) for match in matches]
+            span = pl.ds(pl.multiple_of(row * cols, cols), cols)
+            acc[...] += jnp.dot(
+                jnp.concatenate(spread, axis=0), hot[span, :], preferred_element_type=jnp.float32
             )
             return carry
 
@@ -666,9 +688,9 @@
         for array in (work, stat):
             for edge in (0, LEAD + span):
                 array[:, edge : edge + LEAD] = jnp.zeros((array.shape[0], LEAD, LANES), jnp.float32)
-        prepare_remap()
         for copy in loads[4:]:
             copy.wait()
+        prepare_remap()
         sent(first)
         sent(second)
         pl.semaphore_signal(go, inc=1, device_id={"comp": 1 - comp}, device_id_type=MESH)
@@ -725,8 +747,9 @@
         mean[2] = forcing[4] * covered * (home[2] * share)
         mean_copy.start()
         pair[...] = mean[...]
+        split_values(mean)
         for half in (1, 0):
-            remap(mean, half)
+            remap(half)
             start(sides[half])
         sent(totals)
         arrive(states)
@@ -785,12 +808,13 @@
         state[:, :, lanes_of(me)] = back[3 : 3 + fields, rows_of(me), :]
         sent(first)
         mean_copy.wait_recv()
-        remap(home, 1)
+        split_values(home)
+        remap(1)
         for channel in range(channels):
             sides[1][channel].wait_recv()
             window[1, channel] += beside[1, channel]
             onward[channel].start()
-        remap(home, 0)
+        remap(0)
         for channel in range(channels):
             sides[0][channel].wait_recv()
             pair[channel] = window[0, channel] + beside[0, channel]
@@ -814,10 +838,7 @@
     dma = pltpu.SemaphoreType.DMA
     return pl.pallas_call(
         tiles_kernel,
-        out_shape=(
-            jax.ShapeDtypeStruct((fields, rows, cols), f32),
-            jax.ShapeDtypeStruct((3, rows, cols), f32),
-        ),
+        out_shape=(pltpu.VMEM((fields, rows, cols), f32), pltpu.VMEM((3, rows, cols), f32)),
         in_specs=[pl.BlockSpec(memory_space=pl.ANY)] * 6,
         out_specs=(vmem, vmem),
         scratch_shapes=[
@@ -839,16 +860,16 @@
             pltpu.VMEM((2, 3, rows, cols), f32),
             pltpu.VMEM((2, 3, rows, cols), f32),
             pltpu.VMEM((3, rows, cols), f32),
-            pltpu.VMEM((low_count, cols), jnp.bfloat16),
-            pltpu.VMEM((high_count, cols), jnp.bfloat16),
+            pltpu.VMEM((rows, cols), f32),
+            pltpu.VMEM((2, rows, cols), f32),
+            pltpu.VMEM((rows * cols, low_count), jnp.bfloat16),
+            pltpu.VMEM((6, rows, cols), f32),
             dma((6,)),
             *[dma((count,)) for _ in range(8)],
             dma, dma, dma((2, 3)), dma((2, 3)), dma((3,)), dma((3,)),
             pltpu.SemaphoreType.REGULAR,
         ],
-        compiler_params=pltpu.CompilerParams(
-            collective_id=0, has_side_effects=True, vmem_limit_bytes=40 * 1024 * 1024
-        ),
+        compiler_params=pltpu.CompilerParams(collective_id=0, has_side_effects=True),
         name="tiles",
     )(initial, forcing, current, cover, targets, weights)
 

time: 54 us -> 48.1 us (0.89)
  local copies, waits for them, and re-layouts: 6.89 us -> 1.4 us
    unnamed x14 -> x2, local copies, waits for them, and re-layouts: 6.89 us -> 1.4 us
where the time goes in v3:
time: 48.1 us; the launch traced here: 47.9 us
  Pallas kernels  45.9 us (95%)
  local copies, waits for them, and re-layouts  1.4 us (3%)
  between operations  0.64 us (1%)
    pallas_call x1, Pallas kernels, run_tiles(): pl.pallas_call(tiles_kernel, out_shape=(pltpu.VMEM((fields, rows, cols),...  45.9 us
    unnamed x2, local copies, waits for them, and re-layouts  1.4 us

profile of v3, /device:TPU:1, one launch (start us, length us, event | category | flops | bytes accessed | tf_op | source)
XLA Modules:
  0.0 47.9 jit_solution(8650410176459715987)
XLA Ops:
  0.6 45.9 %tiles.1 = (f32[5,8,2048]{2,1,0:T(8,128)S(1)}, f32[3,8,2048]{2,1,0:T(8,128)S(1)}) custom-call(f32[5,8,2048]{2,1,0:T(8,128)} %bitcast.5, f32[5,8,2048]{2,1,0:T(8,128)} %forcing_in.1, f32[2,8,2048]{2,1,0:T(8,128)} %current_in.1, s32[8,2048]{1,0:T(8,128)} %cover_in.1, s32[2,8,2048]{2,1,0:T(8,128)} %targets_in.1, s32[2,8,2048]{2,1,0:T(8,128)} %weights_in.1), custom_call_target="tpu_custom_call" | custom-call | tf_op jit(solution)/shard_map/tiles/pallas_call | solution.py:839
  46.5 0.7 %copy.10 = f32[1,5,8,2048]{3,2,1,0:T(8,128)} copy(f32[1,5,8,2048]{3,2,1,0:T(8,128)S(1)} %bitcast.3) | data formatting | bytes 655360
  47.2 0.7 %copy.11 = f32[1,3,8,2048]{3,2,1,0:T(8,128)} copy(f32[1,3,8,2048]{3,2,1,0:T(8,128)S(1)} %bitcast.4) | data formatting | bytes 393216

commit v4 on v3

--- a/solution.py
+++ b/solution.py
@@ -478,7 +478,7 @@
         pl.semaphore_signal(barrier, inc=1, device_id=where, device_id_type=MESH)
 
     def other(step):
-        return lax.rem(me + step, count)
+        return lax.bitwise_xor(me, step)
 
     steps = range(1, count)
     for step in steps:
@@ -518,16 +518,26 @@
             for step in steps
         ]
 
+    def home_copy(source, target, sems, step):
+        return pltpu.make_async_remote_copy(
+            source.at[:, rows_of(other(step)), :],
+            target.at[:, :, lanes_of(me)],
+            sems[0].at[step], sems[1].at[step],
+            device_id={"blk": other(step)}, device_id_type=MESH,
+        )
+
     def homeward(source, target, sems):
-        return [
-            pltpu.make_async_remote_copy(
-                source.at[:, rows_of(other(step)), :],
-                target.at[:, :, lanes_of(me)],
-                sems[0].at[step], sems[1].at[step],
-                device_id={"blk": other(step)}, device_id_type=MESH,
-            )
-            for step in steps
-        ]
+        return [home_copy(source, target, sems, step) for step in steps]
+
+    width = hot.shape[1]
+    members = width // LANES
+    chunks = cols // width
+
+    def chunk_of(turn):
+        return lax.bitwise_xor(lax.div(me, members), turn)
+
+    def span_of(turn):
+        return pl.ds(pl.multiple_of(chunk_of(turn) * width, width), width)
 
     def start(copies):
         for copy in copies:
@@ -575,10 +585,13 @@
         )
 
     channels = pair.shape[0]
-    mean_copy = pltpu.make_async_remote_copy(
-        mean, home, mean_send, mean_recv,
-        device_id={"comp": 1 - comp}, device_id_type=MESH,
-    )
+
+    def mean_copy(turn):
+        return pltpu.make_async_remote_copy(
+            mean.at[:, :, span_of(turn)], home.at[:, :, span_of(turn)],
+            mean_send.at[turn], mean_recv.at[turn],
+            device_id={"comp": 1 - comp}, device_id_type=MESH,
+        )
     sides = [
         [
             pltpu.make_async_remote_copy(
@@ -594,74 +607,90 @@
         pltpu.make_async_remote_copy(
             window.at[1, channel], before.at[channel],
             next_send.at[channel], next_recv.at[channel],
-            device_id={"blk": other(1)}, device_id_type=MESH,
+            device_id={"blk": lax.rem(me + 1, count)}, device_id_type=MESH,
         )
         for channel in range(channels)
     ]
 
     def prepare_remap():
-        low_count = hot.shape[1]
-        blocks = cols // low_count
         target = targets[...]
-        block = lax.rem(lax.div(target, low_count), blocks)
+        block = lax.rem(lax.div(target, width), chunks)
         line = lax.div(target, cols)
-        low[...] = lax.rem(target, low_count).astype(jnp.float32)
+        low[...] = lax.rem(target, width).astype(jnp.float32)
         for half in range(2):
             inside = lax.div(line, rows) == half
             place = block * rows + line - half * rows
-            high[half] = jnp.where(inside, place, blocks * rows).astype(jnp.float32)
+            high[half] = jnp.where(inside, place, chunks * rows).astype(jnp.float32)
+        acc[...] = jnp.zeros_like(acc)
 
         def one_row(row, carry):
             lane = lane_index((LANES, LANES)).astype(jnp.float32)
             line = low[pl.ds(row, 1), :]
             for start in range(0, cols, LANES):
                 value = jnp.broadcast_to(line[:, start : start + LANES], (LANES, LANES)).T
-                place = pl.ds(pl.multiple_of(row * cols + start, LANES), LANES)
-                for first in range(0, low_count, LANES):
+                base = start // width * rows * width + start % width
+                place = pl.ds(pl.multiple_of(base + row * width, LANES), LANES)
+                for first in range(0, width, LANES):
                     hit = jnp.where(value == lane + float(first), 1.0, 0.0)
                     hot[place, first : first + LANES] = hit.astype(hot.dtype)
             return carry
 
         lax.fori_loop(0, rows, one_row, 0)
 
-    def split_values(values):
-        scale = weights[...].astype(jnp.float32) * (1.0 / weight_norm)
+    def split_values(values, turn):
+        span = span_of(turn)
+        scale = weights[:, span].astype(jnp.float32) * (1.0 / weight_norm)
         for channel in range(channels):
-            value = values[channel] * scale
+            value = values[channel, :, span] * scale
             coarse = value.astype(jnp.bfloat16).astype(jnp.float32)
-            parts[2 * channel] = coarse
-            parts[2 * channel + 1] = value - coarse
-
-    def remap(half):
-        low_count = hot.shape[1]
-        blocks = cols // low_count
-        high_count = blocks * rows
+            parts[2 * channel, :, span] = coarse
+            parts[2 * channel + 1, :, span] = value - coarse
+
+    def remap(half, turn):
         bf16 = jnp.bfloat16
         tall = 16
-        acc[...] = jnp.zeros_like(acc)
-
-        def one_row(row, carry):
-            place = pl.ds(row, 1)
-            level = jnp.broadcast_to(high[half, place, :], (tall, cols)).astype(bf16)
-            index = lax.broadcasted_iota(jnp.int32, (tall, cols), 0).astype(bf16)
-            matches = [level == index + bf16(first) for first in range(0, high_count, tall)]
-            spread = []
-            for part in range(2 * channels):
-                value = jnp.broadcast_to(parts[part, place, :], (tall, cols)).astype(bf16)
-                spread += [jnp.where(match, value, bf16(0)) for match in matches]
-            span = pl.ds(pl.multiple_of(row * cols, cols), cols)
-            acc[...] += jnp.dot(
-                jnp.concatenate(spread, axis=0), hot[span, :], preferred_element_type=jnp.float32
-            )
+        span = span_of(turn)
+        index = lax.broadcasted_iota(jnp.int32, (tall, width), 0).astype(bf16)
+
+        def lines(block):
+            return [
+                jnp.broadcast_to(block[row : row + 1], (tall, width)).astype(bf16)
+                for row in range(rows)
+            ]
+
+        levels = lines(high[half, :, span])
+        matches = [
+            [level == index + bf16(first) for level in levels]
+            for first in range(0, chunks * rows, tall)
+        ]
+        spread = []
+        for part in range(2 * channels):
+            values = lines(parts[part, :, span])
+            for match in matches:
+                kept = [jnp.where(m, v, bf16(0)) for m, v in zip(match, values)]
+                spread.append(jnp.concatenate(kept, axis=1))
+        depth = rows * width
+        place = pl.ds(pl.multiple_of(chunk_of(turn) * depth, depth), depth)
+        acc[half] += jnp.dot(
+            jnp.concatenate(spread, axis=0), hot[place, :], preferred_element_type=jnp.float32
+        )
+
+    def gather_window(half):
+        tall = chunks * rows
+        for channel in range(channels):
+            for block in range(chunks):
+                base = 2 * channel * tall + block * rows
+                window[half, channel, :, block * width : (block + 1) * width] = (
+                    acc[half, base : base + rows] + acc[half, base + tall : base + tall + rows]
+                )
+
+    def lower_half():
+        def one_chunk(turn, carry):
+            remap(0, turn)
             return carry
 
-        lax.fori_loop(0, rows, one_row, 0)
-        for channel in range(channels):
-            for block in range(blocks):
-                base = 2 * channel * high_count + block * rows
-                window[half, channel, :, block * low_count : (block + 1) * low_count] = (
-                    acc[base : base + rows] + acc[base + high_count : base + high_count + rows]
-                )
+        lax.fori_loop(0, chunks, one_chunk, 0, unroll=4)
+        gather_window(0)
 
     @pl.when(comp == 0)
     def _():
@@ -740,21 +769,35 @@
         home[:, :, lanes_of(me)] = back[0:3, rows_of(me), :]
         state[:, :, lanes_of(me)] = back[3 : 3 + fields, rows_of(me), :]
         share = 1.0 / SUBCYCLES
-        covered = cover[...].astype(jnp.float32)
-        arrive(totals)
-        mean[0] = home[0] * share - covered * current[0]
-        mean[1] = home[1] * share - covered * current[1]
-        mean[2] = forcing[4] * covered * (home[2] * share)
-        mean_copy.start()
+        def upper_chunk(turn, carry):
+            for place in range(members):
+                step = turn * members + place
+
+                @pl.when(step > 0)
+                def _():
+                    home_copy(back.at[0:3], home, (total_send, total_recv), step).wait_recv()
+
+            span = span_of(turn)
+            covered = cover[:, span].astype(jnp.float32)
+            for axis in range(2):
+                mean[axis, :, span] = home[axis, :, span] * share - covered * current[axis, :, span]
+            mean[2, :, span] = forcing[4, :, span] * covered * (home[2, :, span] * share)
+            mean_copy(turn).start()
+            split_values(mean, turn)
+            remap(1, turn)
+            return carry
+
+        lax.fori_loop(0, chunks, upper_chunk, 0)
+        gather_window(1)
+        start(sides[1])
         pair[...] = mean[...]
-        split_values(mean)
-        for half in (1, 0):
-            remap(half)
-            start(sides[half])
+        lower_half()
+        start(sides[0])
         sent(totals)
         arrive(states)
         sent(states)
-        mean_copy.wait_send()
+        for turn in range(chunks):
+            mean_copy(turn).wait_send()
         sent(sides[0] + sides[1])
 
     @pl.when(comp == 1)
@@ -807,14 +850,19 @@
         start(states)
         state[:, :, lanes_of(me)] = back[3 : 3 + fields, rows_of(me), :]
         sent(first)
-        mean_copy.wait_recv()
-        split_values(home)
-        remap(1)
+        def upper_chunk(turn, carry):
+            mean_copy(turn).wait_recv()
+            split_values(home, turn)
+            remap(1, turn)
+            return carry
+
+        lax.fori_loop(0, chunks, upper_chunk, 0)
+        gather_window(1)
         for channel in range(channels):
             sides[1][channel].wait_recv()
             window[1, channel] += beside[1, channel]
             onward[channel].start()
-        remap(0)
+        lower_half()
         for channel in range(channels):
             sides[0][channel].wait_recv()
             pair[channel] = window[0, channel] + beside[0, channel]
@@ -856,7 +904,7 @@
             pltpu.VMEM((3 + fields, LANES, LANES), f32),
             pltpu.VMEM((3, rows, cols), f32),
             pltpu.VMEM((3, rows, cols), f32),
-            pltpu.VMEM((6 * high_count, low_count), f32),
+            pltpu.VMEM((2, 6 * high_count, low_count), f32),
             pltpu.VMEM((2, 3, rows, cols), f32),
             pltpu.VMEM((2, 3, rows, cols), f32),
             pltpu.VMEM((3, rows, cols), f32),
@@ -866,7 +914,7 @@
             pltpu.VMEM((6, rows, cols), f32),
             dma((6,)),
             *[dma((count,)) for _ in range(8)],
-            dma, dma, dma((2, 3)), dma((2, 3)), dma((3,)), dma((3,)),
+            dma((cols // low_count,)), dma((cols // low_count,)), dma((2, 3)), dma((2, 3)), dma((3,)), dma((3,)),
             pltpu.SemaphoreType.REGULAR,
         ],
         compiler_params=pltpu.CompilerParams(collective_id=0, has_side_effects=True),

time: 48.1 us -> 43.8 us (0.911)
  Pallas kernels: 45.9 us -> 41.6 us
    pallas_call x1, Pallas kernels: 45.9 us -> 41.6 us  [run_tiles(): pl.pallas_call(tiles_kernel, out_shape=(pltpu.VMEM((fields, rows, cols),...]
where the time goes in v4:
time: 43.8 us; the launch traced here: 43.7 us
  Pallas kernels  41.6 us (95%)
  local copies, waits for them, and re-layouts  1.4 us (3%)
  between operations  0.64 us (1%)
    pallas_call x1, Pallas kernels, run_tiles(): pl.pallas_call(tiles_kernel, out_shape=(pltpu.VMEM((fields, rows, cols),...  41.6 us
    unnamed x2, local copies, waits for them, and re-layouts  1.4 us

profile of v4, /device:TPU:1, one launch (start us, length us, event | category | flops | bytes accessed | tf_op | source)
XLA Modules:
  0.0 43.7 jit_solution(12505345076768270731)
XLA Ops:
  0.6 41.6 %tiles.1 = (f32[5,8,2048]{2,1,0:T(8,128)S(1)}, f32[3,8,2048]{2,1,0:T(8,128)S(1)}) custom-call(f32[5,8,2048]{2,1,0:T(8,128)} %bitcast.5, f32[5,8,2048]{2,1,0:T(8,128)} %forcing_in.1, f32[2,8,2048]{2,1,0:T(8,128)} %current_in.1, s32[8,2048]{1,0:T(8,128)} %cover_in.1, s32[2,8,2048]{2,1,0:T(8,128)} %targets_in.1, s32[2,8,2048]{2,1,0:T(8,128)} %weights_in.1), custom_call_target="tpu_custom_call" | custom-call | tf_op jit(solution)/shard_map/tiles/pallas_call | solution.py:887
  42.3 0.7 %copy.10 = f32[1,5,8,2048]{3,2,1,0:T(8,128)} copy(f32[1,5,8,2048]{3,2,1,0:T(8,128)S(1)} %bitcast.3) | data formatting | bytes 655360
  43.0 0.7 %copy.11 = f32[1,3,8,2048]{3,2,1,0:T(8,128)} copy(f32[1,3,8,2048]{3,2,1,0:T(8,128)S(1)} %bitcast.4) | data formatting | bytes 393216

commit v5 on v4

--- a/solution.py
+++ b/solution.py
@@ -410,27 +410,24 @@
 
 def tile_stress(work, stat, low, size):
     here, up, down = (pl.ds(low + shift, size) for shift in (0, 1, -1))
-    vel_x, vel_y = work[0, here], work[1, here]
     cx = work[0, up] - work[0, down]
     cy = work[1, up] - work[1, down]
-    rx, ry = lane_diff(vel_x), lane_diff(vel_y)
+    rx, ry = lane_diff(work[0, here]), lane_diff(work[1, here])
     e_d = rx + cy
     e_t = rx - cy
     e_s = cx + ry
-    inv = lax.rsqrt(0.25 * (e_d * e_d) + 0.0625 * (e_t * e_t + e_s * e_s) + 0.01)
-    third = stat[0, here]
-    scaled = third * inv
-    one = 0.5 * scaled * e_d - third
-    two = 0.125 * scaled * e_t
-    work[2, here] = work[2, here] * (2.0 / 3.0) + (one + two)
-    work[3, here] = work[3, here] * (2.0 / 3.0) + (one - two)
-    work[4, here] = work[4, here] * (2.0 / 3.0) + 0.0625 * scaled * e_s
+    fourfold = 4.0 * e_d
+    scaled = stat[0, here] * lax.rsqrt(fourfold * e_d + (e_t * e_t + e_s * e_s) + 0.16)
+    rest = stat[5, here]
+    work[2, here] = work[2, here] * (2.0 / 3.0) + (scaled * (fourfold + e_t) - rest)
+    work[3, here] = work[3, here] * (2.0 / 3.0) + (scaled * (fourfold - e_t) - rest)
+    work[4, here] = work[4, here] * (2.0 / 3.0) + scaled * e_s
 
 
 def tile_velocity(work, stat, total, low, size, own):
     here, up, down = (pl.ds(low + shift, size) for shift in (0, 1, -1))
-    force_x = lane_diff(work[2, here]) + 2.0 * (work[4, up] - work[4, down])
-    force_y = 2.0 * lane_diff(work[4, here]) + (work[3, up] - work[3, down])
+    force_x = lane_diff(work[2, here]) + (work[4, up] - work[4, down])
+    force_y = lane_diff(work[4, here]) + (work[3, up] - work[3, down])
     old_x, old_y = work[0, here], work[1, here]
     keep, push = stat[1, here], stat[2, here]
     new_x = keep * (old_x + coriolis * old_y) + push * force_x + stat[3, here]
@@ -466,7 +463,7 @@
     low, high, hot, parts,
     load, first_send, first_recv, second_send, second_recv,
     total_send, total_recv, state_send, state_recv, mean_send, mean_recv,
-    side_send, side_recv, next_send, next_recv, go,
+    side_send, side_recv, next_send, next_recv, edge_send, edge_recv, go,
 ):
     me = lax.axis_index("blk")
     comp = lax.axis_index("comp")
@@ -501,6 +498,22 @@
     for copy in loads:
         copy.start()
 
+    turn_size = min(4, count)
+
+    def mirrored(group, place):
+        return place + lax.rem(group, 2) * (turn_size - 1 - 2 * place)
+
+    def column_of(device):
+        group, place = lax.div(device, turn_size), lax.rem(device, turn_size)
+        return group * turn_size + mirrored(group, lax.bitwise_xor(place, lax.div(place, 2)))
+
+    def device_of(column):
+        group, place = lax.div(column, turn_size), lax.rem(column, turn_size)
+        place = mirrored(group, place)
+        return group * turn_size + lax.bitwise_xor(place, lax.div(place, 2))
+
+    mine = column_of(me)
+
     def lanes_of(block):
         return pl.ds(pl.multiple_of(block * LANES, LANES), LANES)
 
@@ -510,7 +523,7 @@
     def outward(low, high, sems):
         return [
             pltpu.make_async_remote_copy(
-                pack.at[low:high, :, lanes_of(other(step))],
+                pack.at[low:high, :, lanes_of(column_of(other(step)))],
                 recv.at[low:high, rows_of(me), :],
                 sems[0].at[step], sems[1].at[step],
                 device_id={"blk": other(step)}, device_id_type=MESH,
@@ -521,7 +534,7 @@
     def home_copy(source, target, sems, step):
         return pltpu.make_async_remote_copy(
             source.at[:, rows_of(other(step)), :],
-            target.at[:, :, lanes_of(me)],
+            target.at[:, :, lanes_of(mine)],
             sems[0].at[step], sems[1].at[step],
             device_id={"blk": other(step)}, device_id_type=MESH,
         )
@@ -534,7 +547,8 @@
     chunks = cols // width
 
     def chunk_of(turn):
-        return lax.bitwise_xor(lax.div(me, members), turn)
+        device = members * lax.bitwise_xor(lax.div(me, members), turn)
+        return lax.div(column_of(device), members)
 
     def span_of(turn):
         return pl.ds(pl.multiple_of(chunk_of(turn) * width, width), width)
@@ -551,14 +565,14 @@
         for copy in copies:
             copy.wait_send()
 
-    def spread_edges(base, filled, reach):
+    def spread_edges(base, low, filled, reach):
         group = LANES // (2 * reach)
         lane = lane_index((rows, LANES))
         slot = lane // (2 * reach)
         leading = lane % (2 * reach) < reach
         zero = jnp.zeros((rows, LANES), jnp.float32)
-        for tile in range(-(-filled // group)):
-            members = range(tile * group, min(filled, (tile + 1) * group))
+        for tile in range(-(-(filled - low) // group)):
+            members = range(low + tile * group, min(filled, low + (tile + 1) * group))
             turned = []
             for block in range(count):
                 here = slice(block * LANES, (block + 1) * LANES)
@@ -575,13 +589,13 @@
                 here = slice(block * LANES, (block + 1) * LANES)
                 pack[base + tile, :, here] = jnp.where(leading, before, after)
 
-    def unpack(field, base, reach):
+    def unpack(field, base, low, reach):
         group = LANES // (2 * reach)
         value = recv[field].T
-        edge = recv[base + field // group].T
-        low = field % group * 2 * reach
+        edge = recv[base + (field - low) // group].T
+        start = (field - low) % group * 2 * reach
         return jnp.concatenate(
-            [edge[low : low + reach], value, edge[low + reach : low + 2 * reach]], axis=0
+            [edge[start : start + reach], value, edge[start + reach : start + 2 * reach]], axis=0
         )
 
     channels = pair.shape[0]
@@ -695,7 +709,7 @@
     @pl.when(comp == 0)
     def _():
         filled = fields + 4
-        packed = filled + -(-filled // (LANES // (2 * ICE_REACH)))
+        packed = filled + -(-4 // (LANES // (2 * ICE_REACH)))
         span = LANES + 2 * ICE_REACH
         loads[0].wait()
         pl.semaphore_wait(barrier, count)
@@ -709,10 +723,10 @@
         pack[fields + 1] = push
         pack[fields + 2] = push * (forcing[2] + current[0])
         pack[fields + 3] = push * (forcing[3] + current[1])
-        spread_edges(filled, filled, ICE_REACH)
+        spread_edges(filled, fields, filled, ICE_REACH)
         second = outward(fields, packed, (second_send, second_recv))
         start(second)
-        recv[0:packed, rows_of(me), :] = pack[0:packed, :, lanes_of(me)]
+        recv[0:packed, rows_of(me), :] = pack[0:packed, :, lanes_of(mine)]
         total[...] = jnp.zeros_like(total)
         for array in (work, stat):
             for edge in (0, LEAD + span):
@@ -720,35 +734,66 @@
         for copy in loads[4:]:
             copy.wait()
         prepare_remap()
+        left, middle, right = LEAD, LEAD + ICE_REACH, LEAD + ICE_REACH + LANES
+        onto_right = pltpu.make_async_remote_copy(
+            work.at[:, right - ICE_REACH : right], work.at[:, left:middle],
+            edge_send.at[0], edge_recv.at[0],
+            device_id={"blk": device_of(lax.rem(mine + 1, count))}, device_id_type=MESH,
+        )
+        onto_left = pltpu.make_async_remote_copy(
+            work.at[:, middle : middle + ICE_REACH], work.at[:, right : right + ICE_REACH],
+            edge_send.at[1], edge_recv.at[1],
+            device_id={"blk": device_of(lax.rem(mine + count - 1, count))}, device_id_type=MESH,
+        )
+        has_left, has_right = mine > 0, mine < count - 1
+        arrive(first)
+        work[0, middle:right] = recv[0].T
+        work[1, middle:right] = recv[1].T
+        one, two = recv[2].T, recv[3].T
+        work[2, middle:right] = 8.0 * (one + two)
+        work[3, middle:right] = 8.0 * (one - two)
+        work[4, middle:right] = 16.0 * recv[4].T
+        pl.when(has_right)(onto_right.start)
+        pl.when(has_left)(onto_left.start)
+
+        blank = jnp.zeros((fields, ICE_REACH, LANES), jnp.float32)
+
+        @pl.when(jnp.logical_not(has_left))
+        def _():
+            work[:, left:middle] = blank
+
+        @pl.when(jnp.logical_not(has_right))
+        def _():
+            work[:, right : right + ICE_REACH] = blank
+
         sent(first)
         sent(second)
         pl.semaphore_signal(go, inc=1, device_id={"comp": 1 - comp}, device_id_type=MESH)
-        arrive(first)
         arrive(second)
         whole = slice(LEAD, LEAD + span)
-        for field in range(2):
-            work[field, whole] = unpack(field, filled, ICE_REACH)
-        one, two = unpack(2, filled, ICE_REACH), unpack(3, filled, ICE_REACH)
-        work[2, whole] = one + two
-        work[3, whole] = one - two
-        work[4, whole] = unpack(4, filled, ICE_REACH)
-        stat[0, whole] = unpack(fields, filled, ICE_REACH)
-        push = unpack(fields + 1, filled, ICE_REACH)
+        third = unpack(fields, filled, fields, ICE_REACH)
+        stat[0, whole] = 4.0 * third
+        stat[5, whole] = 8.0 * third
+        push = unpack(fields + 1, filled, fields, ICE_REACH)
         stat[1, whole] = jnp.where(push > 0.0, 1.0 - push, 0.0)
-        stat[2, whole] = 0.25 * push
-        stat[3, whole] = unpack(fields + 2, filled, ICE_REACH)
-        stat[4, whole] = unpack(fields + 3, filled, ICE_REACH)
+        stat[2, whole] = (0.25 / 8.0) * push
+        stat[3, whole] = unpack(fields + 2, filled, fields, ICE_REACH)
+        stat[4, whole] = unpack(fields + 3, filled, fields, ICE_REACH)
+        pl.when(has_left)(onto_right.wait_recv)
+        pl.when(has_right)(onto_left.wait_recv)
+        pl.when(has_right)(onto_right.wait_send)
+        pl.when(has_left)(onto_left.wait_send)
 
         for group in range(SUBCYCLES // 4):
             low, high = LEAD + 8 * group, LEAD + span - 8 * group
             inner, outer = LEAD + ICE_REACH, LEAD + ICE_REACH + LANES
 
             def subcycle(step, carry, low=low, high=high):
-                for begin, size in pieces(low, high, 16):
+                for begin, size in pieces(low, high, 8):
                     tile_stress(work, stat, begin, size)
-                for begin, size in pieces(low, inner, 16) + pieces(outer, high, 16):
+                for begin, size in pieces(low, inner, 8) + pieces(outer, high, 8):
                     tile_velocity(work, stat, total, begin, size, None)
-                for begin, size in pieces(inner, outer, 16):
+                for begin, size in pieces(inner, outer, 8):
                     tile_velocity(work, stat, total, begin, size, begin - inner)
                 return carry
 
@@ -761,13 +806,19 @@
         start(totals)
         one, two = work[2, own], work[3, own]
         for field, value in enumerate(
-            (work[0, own], work[1, own], 0.5 * (one + two), 0.5 * (one - two), work[4, own])
+            (
+                work[0, own],
+                work[1, own],
+                (0.5 / 8.0) * (one + two),
+                (0.5 / 8.0) * (one - two),
+                (1.0 / 16.0) * work[4, own],
+            )
         ):
             back[3 + field] = value.T
         states = homeward(back.at[3 : 3 + fields], state, (state_send, state_recv))
         start(states)
-        home[:, :, lanes_of(me)] = back[0:3, rows_of(me), :]
-        state[:, :, lanes_of(me)] = back[3 : 3 + fields, rows_of(me), :]
+        home[:, :, lanes_of(mine)] = back[0:3, rows_of(me), :]
+        state[:, :, lanes_of(mine)] = back[3 : 3 + fields, rows_of(me), :]
         share = 1.0 / SUBCYCLES
         def upper_chunk(turn, carry):
             for place in range(members):
@@ -809,11 +860,11 @@
             copy.wait()
         for axis in range(2):
             pack[fields + axis] = current[axis]
-        spread_edges(filled, filled, SEA_REACH)
+        spread_edges(filled, 0, filled, SEA_REACH)
         for array in (work, spare):
             for edge in (0, LEAD + span):
                 array[:, edge : edge + LEAD] = jnp.zeros((array.shape[0], LEAD, LANES), jnp.float32)
-        recv[0:packed, rows_of(me), :] = pack[0:packed, :, lanes_of(me)]
+        recv[0:packed, rows_of(me), :] = pack[0:packed, :, lanes_of(mine)]
         prepare_remap()
         pl.semaphore_wait(barrier, count)
         pl.semaphore_wait(go, 1)
@@ -822,13 +873,13 @@
         arrive(first)
         whole = slice(LEAD, LEAD + span)
         for field in range(fields):
-            work[field, whole] = unpack(field, filled, SEA_REACH)
+            work[field, whole] = unpack(field, filled, 0, SEA_REACH)
         lane = lane_index((span, LANES))
-        speed = courant * unpack(fields, filled, SEA_REACH)
+        speed = courant * unpack(fields, filled, 0, SEA_REACH)
         drain = jnp.abs(speed)
         stat[0, whole] = jnp.where(lane == 0, 0.0, jnp.maximum(speed, 0.0))
         stat[1, whole] = jnp.where(lane == LANES - 1, 0.0, -jnp.minimum(speed, 0.0))
-        speed = courant * unpack(fields + 1, filled, SEA_REACH)
+        speed = courant * unpack(fields + 1, filled, 0, SEA_REACH)
         stat[2, whole] = jnp.maximum(speed, 0.0)
         stat[3, whole] = -jnp.minimum(speed, 0.0)
         stat[4, whole] = drain + jnp.abs(speed)
@@ -848,7 +899,7 @@
             back[3 + field] = work[field, own].T
         states = homeward(back.at[3 : 3 + fields], state, (state_send, state_recv))
         start(states)
-        state[:, :, lanes_of(me)] = back[3 : 3 + fields, rows_of(me), :]
+        state[:, :, lanes_of(mine)] = back[3 : 3 + fields, rows_of(me), :]
         sent(first)
         def upper_chunk(turn, carry):
             mean_copy(turn).wait_recv()
@@ -878,7 +929,7 @@
     fields, rows, cols = initial.shape
     f32 = jnp.float32
     most = fields + 4
-    packed = most + -(-most // (LANES // (2 * ICE_REACH)))
+    packed = most + -(-4 // (LANES // (2 * ICE_REACH)))
     tall = LANES + 2 * ICE_REACH + 2 * LEAD
     low_count = 256 if cols % 256 == 0 else 128
     high_count = rows * cols // low_count
@@ -899,7 +950,7 @@
             pltpu.VMEM((packed, LANES, LANES), f32),
             pltpu.VMEM((fields, tall, LANES), f32),
             pltpu.VMEM((fields, tall, LANES), f32),
-            pltpu.VMEM((5, tall, LANES), f32),
+            pltpu.VMEM((6, tall, LANES), f32),
             pltpu.VMEM((3, LANES, LANES), f32),
             pltpu.VMEM((3 + fields, LANES, LANES), f32),
             pltpu.VMEM((3, rows, cols), f32),
@@ -914,7 +965,7 @@
             pltpu.VMEM((6, rows, cols), f32),
             dma((6,)),
             *[dma((count,)) for _ in range(8)],
-            dma((cols // low_count,)), dma((cols // low_count,)), dma((2, 3)), dma((2, 3)), dma((3,)), dma((3,)),
+            dma((cols // low_count,)), dma((cols // low_count,)), dma((2, 3)), dma((2, 3)), dma((3,)), dma((3,)), dma((2,)), dma((2,)),
             pltpu.SemaphoreType.REGULAR,
         ],
         compiler_params=pltpu.CompilerParams(collective_id=0, has_side_effects=True),

time: 43.8 us -> 42.7 us (0.975)
  Pallas kernels: 41.6 us -> 40.5 us
    pallas_call x1, Pallas kernels: 41.6 us -> 40.5 us  [run_tiles(): pl.pallas_call(tiles_kernel, out_shape=(pltpu.VMEM((fields, rows, cols),...]
where the time goes in v5:
time: 42.7 us; the launch traced here: 42.6 us
  Pallas kernels  40.5 us (95%)
  local copies, waits for them, and re-layouts  1.4 us (3%)
  between operations  0.64 us (1%)
    pallas_call x1, Pallas kernels, run_tiles(): pl.pallas_call(tiles_kernel, out_shape=(pltpu.VMEM((fields, rows, cols),...  40.5 us
    unnamed x2, local copies, waits for them, and re-layouts  1.4 us

profile of v5, /device:TPU:1, one launch (start us, length us, event | category | flops | bytes accessed | tf_op | source)
XLA Modules:
  0.0 42.6 jit_solution(1221158004516012994)
XLA Ops:
  0.6 40.5 %tiles.1 = (f32[5,8,2048]{2,1,0:T(8,128)S(1)}, f32[3,8,2048]{2,1,0:T(8,128)S(1)}) custom-call(f32[5,8,2048]{2,1,0:T(8,128)} %bitcast.5, f32[5,8,2048]{2,1,0:T(8,128)} %forcing_in.1, f32[2,8,2048]{2,1,0:T(8,128)} %current_in.1, s32[8,2048]{1,0:T(8,128)} %cover_in.1, s32[2,8,2048]{2,1,0:T(8,128)} %targets_in.1, s32[2,8,2048]{2,1,0:T(8,128)} %weights_in.1), custom_call_target="tpu_custom_call" | custom-call | tf_op jit(solution)/shard_map/tiles/pallas_call | solution.py:938
  41.2 0.7 %copy.10 = f32[1,5,8,2048]{3,2,1,0:T(8,128)} copy(f32[1,5,8,2048]{3,2,1,0:T(8,128)S(1)} %bitcast.3) | data formatting | bytes 655360
  41.9 0.7 %copy.11 = f32[1,3,8,2048]{3,2,1,0:T(8,128)} copy(f32[1,3,8,2048]{3,2,1,0:T(8,128)S(1)} %bitcast.4) | data formatting | bytes 393216

commit v6 on v5

--- a/solution.py
+++ b/solution.py
@@ -525,26 +525,33 @@
             pltpu.make_async_remote_copy(
                 pack.at[low:high, :, lanes_of(column_of(other(step)))],
                 recv.at[low:high, rows_of(me), :],
-                sems[0].at[step], sems[1].at[step],
+                sems[0], sems[1],
                 device_id={"blk": other(step)}, device_id_type=MESH,
             )
             for step in steps
         ]
 
+    width = hot.shape[1]
+    members = width // LANES
+    chunks = cols // width
+
     def home_copy(source, target, sems, step):
         return pltpu.make_async_remote_copy(
             source.at[:, rows_of(other(step)), :],
             target.at[:, :, lanes_of(mine)],
-            sems[0].at[step], sems[1].at[step],
+            sems[0], sems[1],
             device_id={"blk": other(step)}, device_id_type=MESH,
         )
 
     def homeward(source, target, sems):
         return [home_copy(source, target, sems, step) for step in steps]
 
-    width = hot.shape[1]
-    members = width // LANES
-    chunks = cols // width
+    def totals_home():
+        return [
+            home_copy(back.at[0:3], home, (total_send, total_recv.at[step // members]), step)
+            for step in steps
+        ]
+
 
     def chunk_of(turn):
         device = members * lax.bitwise_xor(lax.div(me, members), turn)
@@ -557,13 +564,17 @@
         for copy in copies:
             copy.start()
 
-    def arrive(copies):
-        for copy in copies:
-            copy.wait_recv()
-
-    def sent(copies):
-        for copy in copies:
-            copy.wait_send()
+    def bulk(block, sems):
+        return pltpu.make_async_remote_copy(
+            block, block, sems[0], sems[1],
+            device_id={"comp": 1 - comp}, device_id_type=MESH,
+        )
+
+    def outward_bulk(low, high, sems):
+        return bulk(recv.at[low:high, 0 : (count - 1) * rows, :], sems)
+
+    def homeward_bulk(low, high, sems):
+        return bulk(back.at[low:high, 0 : (count - 1) * rows, :], sems)
 
     def spread_edges(base, low, filled, reach):
         group = LANES // (2 * reach)
@@ -603,14 +614,14 @@
     def mean_copy(turn):
         return pltpu.make_async_remote_copy(
             mean.at[:, :, span_of(turn)], home.at[:, :, span_of(turn)],
-            mean_send.at[turn], mean_recv.at[turn],
+            mean_send, mean_recv.at[turn],
             device_id={"comp": 1 - comp}, device_id_type=MESH,
         )
     sides = [
         [
             pltpu.make_async_remote_copy(
                 window.at[half, channel], beside.at[half, channel],
-                side_send.at[half, channel], side_recv.at[half, channel],
+                side_send, side_recv.at[half, channel],
                 device_id={"comp": 1 - comp}, device_id_type=MESH,
             )
             for channel in range(channels)
@@ -620,7 +631,7 @@
     onward = [
         pltpu.make_async_remote_copy(
             window.at[1, channel], before.at[channel],
-            next_send.at[channel], next_recv.at[channel],
+            next_send, next_recv,
             device_id={"blk": lax.rem(me + 1, count)}, device_id_type=MESH,
         )
         for channel in range(channels)
@@ -713,8 +724,7 @@
         span = LANES + 2 * ICE_REACH
         loads[0].wait()
         pl.semaphore_wait(barrier, count)
-        first = outward(0, fields, (first_send, first_recv))
-        start(first)
+        start(outward(0, fields, (first_send, first_recv)))
         for copy in loads[1:4]:
             copy.wait()
         covered = cover[...].astype(jnp.float32)
@@ -724,8 +734,7 @@
         pack[fields + 2] = push * (forcing[2] + current[0])
         pack[fields + 3] = push * (forcing[3] + current[1])
         spread_edges(filled, fields, filled, ICE_REACH)
-        second = outward(fields, packed, (second_send, second_recv))
-        start(second)
+        start(outward(fields, packed, (second_send, second_recv)))
         recv[0:packed, rows_of(me), :] = pack[0:packed, :, lanes_of(mine)]
         total[...] = jnp.zeros_like(total)
         for array in (work, stat):
@@ -746,7 +755,7 @@
             device_id={"blk": device_of(lax.rem(mine + count - 1, count))}, device_id_type=MESH,
         )
         has_left, has_right = mine > 0, mine < count - 1
-        arrive(first)
+        outward_bulk(0, fields, (first_send, first_recv)).wait_recv()
         work[0, middle:right] = recv[0].T
         work[1, middle:right] = recv[1].T
         one, two = recv[2].T, recv[3].T
@@ -766,10 +775,11 @@
         def _():
             work[:, right : right + ICE_REACH] = blank
 
-        sent(first)
-        sent(second)
+        outward_bulk(0, fields, (first_send, first_recv)).wait_send()
+        rest = outward_bulk(fields, packed, (second_send, second_recv))
+        rest.wait_send()
         pl.semaphore_signal(go, inc=1, device_id={"comp": 1 - comp}, device_id_type=MESH)
-        arrive(second)
+        rest.wait_recv()
         whole = slice(LEAD, LEAD + span)
         third = unpack(fields, filled, fields, ICE_REACH)
         stat[0, whole] = 4.0 * third
@@ -802,8 +812,7 @@
         own = slice(LEAD + ICE_REACH, LEAD + ICE_REACH + LANES)
         for channel in range(3):
             back[channel] = total[channel].T
-        totals = homeward(back.at[0:3], home, (total_send, total_recv))
-        start(totals)
+        start(totals_home())
         one, two = work[2, own], work[3, own]
         for field, value in enumerate(
             (
@@ -815,18 +824,22 @@
             )
         ):
             back[3 + field] = value.T
-        states = homeward(back.at[3 : 3 + fields], state, (state_send, state_recv))
-        start(states)
+        start(homeward(back.at[3 : 3 + fields], state, (state_send, state_recv)))
         home[:, :, lanes_of(mine)] = back[0:3, rows_of(me), :]
         state[:, :, lanes_of(mine)] = back[3 : 3 + fields, rows_of(me), :]
         share = 1.0 / SUBCYCLES
         def upper_chunk(turn, carry):
-            for place in range(members):
-                step = turn * members + place
-
-                @pl.when(step > 0)
+            sems = (total_send, total_recv.at[turn])
+
+            @pl.when(turn > 0)
+            def _():
+                bulk(home.at[:, :, 0:width], sems).wait_recv()
+
+            if members > 1:
+
+                @pl.when(turn == 0)
                 def _():
-                    home_copy(back.at[0:3], home, (total_send, total_recv), step).wait_recv()
+                    bulk(home.at[:, :, 0 : width - LANES], sems).wait_recv()
 
             span = span_of(turn)
             covered = cover[:, span].astype(jnp.float32)
@@ -844,13 +857,12 @@
         pair[...] = mean[...]
         lower_half()
         start(sides[0])
-        sent(totals)
-        arrive(states)
-        sent(states)
-        for turn in range(chunks):
-            mean_copy(turn).wait_send()
-        sent(sides[0] + sides[1])
-
+        homeward_bulk(0, 3, (total_send, total_recv.at[0])).wait_send()
+        states = homeward_bulk(3, 3 + fields, (state_send, state_recv))
+        states.wait_recv()
+        states.wait_send()
+        bulk(mean, (mean_send, mean_recv.at[0])).wait_send()
+        bulk(window, (side_send, side_recv.at[0, 0])).wait_send()
     @pl.when(comp == 1)
     def _():
         filled = fields + 2
@@ -868,9 +880,8 @@
         prepare_remap()
         pl.semaphore_wait(barrier, count)
         pl.semaphore_wait(go, 1)
-        first = outward(0, packed, (first_send, first_recv))
-        start(first)
-        arrive(first)
+        start(outward(0, packed, (first_send, first_recv)))
+        outward_bulk(0, packed, (first_send, first_recv)).wait_recv()
         whole = slice(LEAD, LEAD + span)
         for field in range(fields):
             work[field, whole] = unpack(field, filled, 0, SEA_REACH)
@@ -897,10 +908,9 @@
         own = slice(LEAD + SEA_REACH, LEAD + SEA_REACH + LANES)
         for field in range(fields):
             back[3 + field] = work[field, own].T
-        states = homeward(back.at[3 : 3 + fields], state, (state_send, state_recv))
-        start(states)
+        start(homeward(back.at[3 : 3 + fields], state, (state_send, state_recv)))
         state[:, :, lanes_of(mine)] = back[3 : 3 + fields, rows_of(me), :]
-        sent(first)
+        outward_bulk(0, packed, (first_send, first_recv)).wait_send()
         def upper_chunk(turn, carry):
             mean_copy(turn).wait_recv()
             split_values(home, turn)
@@ -917,12 +927,38 @@
         for channel in range(channels):
             sides[0][channel].wait_recv()
             pair[channel] = window[0, channel] + beside[0, channel]
-        arrive(states)
-        arrive(onward)
+        states = homeward_bulk(3, 3 + fields, (state_send, state_recv))
+        states.wait_recv()
+        bulk(before, (next_send, next_recv)).wait_recv()
         pair[...] += before[...]
         state[0] -= dilution * pair[2]
-        sent(states)
-        sent(onward)
+        states.wait_send()
+        bulk(before, (next_send, next_recv)).wait_send()
+
+def deliver_kernel(state, pair, out_state, out_pair, sems):
+    copies = [
+        pltpu.make_async_copy(state, out_state, sems.at[0]),
+        pltpu.make_async_copy(pair, out_pair, sems.at[1]),
+    ]
+    for copy in copies:
+        copy.start()
+    for copy in copies:
+        copy.wait()
+
+
+def deliver(state, pair):
+    return pl.pallas_call(
+        deliver_kernel,
+        out_shape=(
+            jax.ShapeDtypeStruct(state.shape, jnp.float32),
+            jax.ShapeDtypeStruct(pair.shape, jnp.float32),
+        ),
+        in_specs=[pl.BlockSpec(memory_space=pltpu.VMEM)] * 2,
+        out_specs=[pl.BlockSpec(memory_space=pl.ANY)] * 2,
+        scratch_shapes=[pltpu.SemaphoreType.DMA((2,))],
+        compiler_params=pltpu.CompilerParams(vmem_limit_bytes=2 * 1024 * 1024),
+        name="deliver",
+    )(state, pair)
 
 
 def run_tiles(initial, forcing, current, cover, targets, weights, count):
@@ -964,8 +1000,9 @@
             pltpu.VMEM((rows * cols, low_count), jnp.bfloat16),
             pltpu.VMEM((6, rows, cols), f32),
             dma((6,)),
-            *[dma((count,)) for _ in range(8)],
-            dma((cols // low_count,)), dma((cols // low_count,)), dma((2, 3)), dma((2, 3)), dma((3,)), dma((3,)), dma((2,)), dma((2,)),
+            *[dma] * 4,
+            dma, dma((cols // low_count,)), dma, dma, dma, dma((cols // low_count,)),
+            dma, dma((2, 3)), dma, dma, dma((2,)), dma((2,)),
             pltpu.SemaphoreType.REGULAR,
         ],
         compiler_params=pltpu.CompilerParams(collective_id=0, has_side_effects=True),
@@ -1129,6 +1166,7 @@
         state, coupled = run_tiles(
             initial[0], ice_forcing, ocean_current, ice_cover, targets, weights, count
         )
+        state, coupled = deliver(state, coupled)
     else:
         state, average = run_turns(initial[0], ice_forcing, ocean_current, ice_cover)
         window = run_remap(average, targets, weights)

time: 42.7 us -> 40.9 us (0.958)
  local copies, waits for them, and re-layouts: 1.4 us -> 0 us
    unnamed x2 -> x0, local copies, waits for them, and re-layouts: 1.4 us -> none
    pallas_call x1, Pallas kernels: 40.5 us -> 39.3 us  [run_tiles(): pl.pallas_call(tiles_kernel, out_shape=(pltpu.VMEM((fields, rows, cols),...]
    pallas_call x0 -> x1, Pallas kernels: none -> 0.8 us  [deliver(): pl.pallas_call(deliver_kernel, out_shape=(jax.ShapeDtypeStruct(state.shap...]
where the time goes in v6:
time: 40.9 us; the launch traced here: 40.8 us
  Pallas kernels  40.2 us (98%)
  between operations  0.64 us (2%)
    pallas_call x1, Pallas kernels, run_tiles(): pl.pallas_call(tiles_kernel, out_shape=(pltpu.VMEM((fields, rows, cols),...  39.3 us

profile of v6, /device:TPU:1, one launch (start us, length us, event | category | flops | bytes accessed | tf_op | source)
XLA Modules:
  0.0 40.8 jit_solution(8791242728138743745)
XLA Ops:
  0.6 39.3 %tiles.1 = (f32[5,8,2048]{2,1,0:T(8,128)S(1)}, f32[3,8,2048]{2,1,0:T(8,128)S(1)}) custom-call(f32[5,8,2048]{2,1,0:T(8,128)} %bitcast.3, f32[5,8,2048]{2,1,0:T(8,128)} %forcing_in.1, f32[2,8,2048]{2,1,0:T(8,128)} %current_in.1, s32[8,2048]{1,0:T(8,128)} %cover_in.1, s32[2,8,2048]{2,1,0:T(8,128)} %targets_in.1, s32[2,8,2048]{2,1,0:T(8,128)} %weights_in.1), custom_call_target="tpu_custom_call" | custom-call | tf_op jit(solution)/shard_map/tiles/pallas_call | solution.py:974
  40.0 0.8 %deliver.1 = (f32[5,8,2048]{2,1,0:T(8,128)}, f32[3,8,2048]{2,1,0:T(8,128)}) custom-call(f32[5,8,2048]{2,1,0:T(8,128)S(1)} %get-tuple-element.6.state, f32[3,8,2048]{2,1,0:T(8,128)S(1)} %get-tuple-element.7.pair), custom_call_target="tpu_custom_call" | custom-call | tf_op jit(solution)/shard_map/deliver/pallas_call | solution.py:950

commit v7 on v6

--- a/solution.py
+++ b/solution.py
@@ -600,6 +600,41 @@
                 here = slice(block * LANES, (block + 1) * LANES)
                 pack[base + tile, :, here] = jnp.where(leading, before, after)
 
+    def edges(reach):
+        left, middle, right = LEAD, LEAD + reach, LEAD + reach + LANES
+        onto_right = pltpu.make_async_remote_copy(
+            work.at[:, right - reach : right], work.at[:, left:middle],
+            edge_send.at[0], edge_recv.at[0],
+            device_id={"blk": device_of(lax.rem(mine + 1, count))}, device_id_type=MESH,
+        )
+        onto_left = pltpu.make_async_remote_copy(
+            work.at[:, middle : middle + reach], work.at[:, right : right + reach],
+            edge_send.at[1], edge_recv.at[1],
+            device_id={"blk": device_of(lax.rem(mine + count - 1, count))}, device_id_type=MESH,
+        )
+        has_left, has_right = mine > 0, mine < count - 1
+        blank = jnp.zeros((fields, reach, LANES), jnp.float32)
+
+        def swap():
+            pl.when(has_right)(onto_right.start)
+            pl.when(has_left)(onto_left.start)
+
+            @pl.when(jnp.logical_not(has_left))
+            def _():
+                work[:, left:middle] = blank
+
+            @pl.when(jnp.logical_not(has_right))
+            def _():
+                work[:, right : right + reach] = blank
+
+        def arrived():
+            pl.when(has_left)(onto_right.wait_recv)
+            pl.when(has_right)(onto_left.wait_recv)
+            pl.when(has_right)(onto_right.wait_send)
+            pl.when(has_left)(onto_left.wait_send)
+
+        return swap, arrived
+
     def unpack(field, base, low, reach):
         group = LANES // (2 * reach)
         value = recv[field].T
@@ -743,18 +778,8 @@
         for copy in loads[4:]:
             copy.wait()
         prepare_remap()
-        left, middle, right = LEAD, LEAD + ICE_REACH, LEAD + ICE_REACH + LANES
-        onto_right = pltpu.make_async_remote_copy(
-            work.at[:, right - ICE_REACH : right], work.at[:, left:middle],
-            edge_send.at[0], edge_recv.at[0],
-            device_id={"blk": device_of(lax.rem(mine + 1, count))}, device_id_type=MESH,
-        )
-        onto_left = pltpu.make_async_remote_copy(
-            work.at[:, middle : middle + ICE_REACH], work.at[:, right : right + ICE_REACH],
-            edge_send.at[1], edge_recv.at[1],
-            device_id={"blk": device_of(lax.rem(mine + count - 1, count))}, device_id_type=MESH,
-        )
-        has_left, has_right = mine > 0, mine < count - 1
+        swap_edges, edges_here = edges(ICE_REACH)
+        middle, right = LEAD + ICE_REACH, LEAD + ICE_REACH + LANES
         outward_bulk(0, fields, (first_send, first_recv)).wait_recv()
         work[0, middle:right] = recv[0].T
         work[1, middle:right] = recv[1].T
@@ -762,19 +787,7 @@
         work[2, middle:right] = 8.0 * (one + two)
         work[3, middle:right] = 8.0 * (one - two)
         work[4, middle:right] = 16.0 * recv[4].T
-        pl.when(has_right)(onto_right.start)
-        pl.when(has_left)(onto_left.start)
-
-        blank = jnp.zeros((fields, ICE_REACH, LANES), jnp.float32)
-
-        @pl.when(jnp.logical_not(has_left))
-        def _():
-            work[:, left:middle] = blank
-
-        @pl.when(jnp.logical_not(has_right))
-        def _():
-            work[:, right : right + ICE_REACH] = blank
-
+        swap_edges()
         outward_bulk(0, fields, (first_send, first_recv)).wait_send()
         rest = outward_bulk(fields, packed, (second_send, second_recv))
         rest.wait_send()
@@ -789,10 +802,7 @@
         stat[2, whole] = (0.25 / 8.0) * push
         stat[3, whole] = unpack(fields + 2, filled, fields, ICE_REACH)
         stat[4, whole] = unpack(fields + 3, filled, fields, ICE_REACH)
-        pl.when(has_left)(onto_right.wait_recv)
-        pl.when(has_right)(onto_left.wait_recv)
-        pl.when(has_right)(onto_right.wait_send)
-        pl.when(has_left)(onto_left.wait_send)
+        edges_here()
 
         for group in range(SUBCYCLES // 4):
             low, high = LEAD + 8 * group, LEAD + span - 8 * group
@@ -866,13 +876,13 @@
     @pl.when(comp == 1)
     def _():
         filled = fields + 2
-        packed = filled + -(-filled // (LANES // (2 * SEA_REACH)))
+        packed = filled + -(-2 // (LANES // (2 * SEA_REACH)))
         span = LANES + 2 * SEA_REACH
         for copy in loads:
             copy.wait()
         for axis in range(2):
             pack[fields + axis] = current[axis]
-        spread_edges(filled, 0, filled, SEA_REACH)
+        spread_edges(filled, fields, filled, SEA_REACH)
         for array in (work, spare):
             for edge in (0, LEAD + span):
                 array[:, edge : edge + LEAD] = jnp.zeros((array.shape[0], LEAD, LANES), jnp.float32)
@@ -880,20 +890,27 @@
         prepare_remap()
         pl.semaphore_wait(barrier, count)
         pl.semaphore_wait(go, 1)
-        start(outward(0, packed, (first_send, first_recv)))
-        outward_bulk(0, packed, (first_send, first_recv)).wait_recv()
+        start(outward(0, fields, (first_send, first_recv)))
+        start(outward(fields, packed, (second_send, second_recv)))
+        swap_edges, edges_here = edges(SEA_REACH)
+        middle, right = LEAD + SEA_REACH, LEAD + SEA_REACH + LANES
+        outward_bulk(0, fields, (first_send, first_recv)).wait_recv()
+        for field in range(fields):
+            work[field, middle:right] = recv[field].T
+        swap_edges()
+        rest = outward_bulk(fields, packed, (second_send, second_recv))
+        rest.wait_recv()
         whole = slice(LEAD, LEAD + span)
-        for field in range(fields):
-            work[field, whole] = unpack(field, filled, 0, SEA_REACH)
         lane = lane_index((span, LANES))
-        speed = courant * unpack(fields, filled, 0, SEA_REACH)
+        speed = courant * unpack(fields, filled, fields, SEA_REACH)
         drain = jnp.abs(speed)
         stat[0, whole] = jnp.where(lane == 0, 0.0, jnp.maximum(speed, 0.0))
         stat[1, whole] = jnp.where(lane == LANES - 1, 0.0, -jnp.minimum(speed, 0.0))
-        speed = courant * unpack(fields + 1, filled, 0, SEA_REACH)
+        speed = courant * unpack(fields + 1, filled, fields, SEA_REACH)
         stat[2, whole] = jnp.maximum(speed, 0.0)
         stat[3, whole] = -jnp.minimum(speed, 0.0)
         stat[4, whole] = drain + jnp.abs(speed)
+        edges_here()
         for group in range(SUBCYCLES // 8):
             low, high = LEAD + 8 * group, LEAD + span - 8 * group
 
@@ -910,7 +927,8 @@
             back[3 + field] = work[field, own].T
         start(homeward(back.at[3 : 3 + fields], state, (state_send, state_recv)))
         state[:, :, lanes_of(mine)] = back[3 : 3 + fields, rows_of(me), :]
-        outward_bulk(0, packed, (first_send, first_recv)).wait_send()
+        outward_bulk(0, fields, (first_send, first_recv)).wait_send()
+        rest.wait_send()
         def upper_chunk(turn, carry):
             mean_copy(turn).wait_recv()
             split_values(home, turn)

time: 40.9 us -> 40.4 us (0.988)
  Pallas kernels: 40.2 us -> 39.6 us
    pallas_call x1, Pallas kernels: 39.3 us -> 38.8 us  [run_tiles(): pl.pallas_call(tiles_kernel, out_shape=(pltpu.VMEM((fields, rows, cols),...]
where the time goes in v7:
time: 40.4 us; the launch traced here: 40.3 us
  Pallas kernels  39.6 us (98%)
  between operations  0.64 us (2%)
    pallas_call x1, Pallas kernels, run_tiles(): pl.pallas_call(tiles_kernel, out_shape=(pltpu.VMEM((fields, rows, cols),...  38.8 us

profile of v7, /device:TPU:1, one launch (start us, length us, event | category | flops | bytes accessed | tf_op | source)
XLA Modules:
  0.0 40.3 jit_solution(2677595923231884427)
XLA Ops:
  0.6 38.8 %tiles.1 = (f32[5,8,2048]{2,1,0:T(8,128)S(1)}, f32[3,8,2048]{2,1,0:T(8,128)S(1)}) custom-call(f32[5,8,2048]{2,1,0:T(8,128)} %bitcast.3, f32[5,8,2048]{2,1,0:T(8,128)} %forcing_in.1, f32[2,8,2048]{2,1,0:T(8,128)} %current_in.1, s32[8,2048]{1,0:T(8,128)} %cover_in.1, s32[2,8,2048]{2,1,0:T(8,128)} %targets_in.1, s32[2,8,2048]{2,1,0:T(8,128)} %weights_in.1), custom_call_target="tpu_custom_call" | custom-call | tf_op jit(solution)/shard_map/tiles/pallas_call | solution.py:992
  39.4 0.8 %deliver.1 = (f32[5,8,2048]{2,1,0:T(8,128)}, f32[3,8,2048]{2,1,0:T(8,128)}) custom-call(f32[5,8,2048]{2,1,0:T(8,128)S(1)} %get-tuple-element.6.state, f32[3,8,2048]{2,1,0:T(8,128)S(1)} %get-tuple-element.7.pair), custom_call_target="tpu_custom_call" | custom-call | tf_op jit(solution)/shard_map/deliver/pallas_call | solution.py:968

commit v8 on v7

--- a/solution.py
+++ b/solution.py
@@ -817,7 +817,7 @@
                     tile_velocity(work, stat, total, begin, size, begin - inner)
                 return carry
 
-            lax.fori_loop(0, 4, subcycle, 0)
+            lax.fori_loop(0, 4, subcycle, 0, unroll=2)
 
         own = slice(LEAD + ICE_REACH, LEAD + ICE_REACH + LANES)
         for channel in range(3):
@@ -921,7 +921,7 @@
                     tile_ocean(spare, work, stat, begin, size)
                 return carry
 
-            lax.fori_loop(0, 4, substeps, 0)
+            lax.fori_loop(0, 4, substeps, 0, unroll=2)
         own = slice(LEAD + SEA_REACH, LEAD + SEA_REACH + LANES)
         for field in range(fields):
             back[3 + field] = work[field, own].T

time: 40.4 us -> 40.1 us (level)
  no operation moved by 1% of the time
where the time goes in v8:
time: 40.1 us; the launch traced here: 40 us
  Pallas kernels  39.3 us (98%)
  between operations  0.64 us (2%)
    pallas_call x1, Pallas kernels, run_tiles(): pl.pallas_call(tiles_kernel, out_shape=(pltpu.VMEM((fields, rows, cols),...  38.5 us
    pallas_call x1, Pallas kernels, deliver(): pl.pallas_call(deliver_kernel, out_shape=(jax.ShapeDtypeStruct(state.shap...  0.8 us

profile of v8, /device:TPU:1, one launch (start us, length us, event | category | flops | bytes accessed | tf_op | source)
XLA Modules:
  0.0 40.0 jit_solution(17450388998637741486)
XLA Ops:
  0.6 38.5 %tiles.1 = (f32[5,8,2048]{2,1,0:T(8,128)S(1)}, f32[3,8,2048]{2,1,0:T(8,128)S(1)}) custom-call(f32[5,8,2048]{2,1,0:T(8,128)} %bitcast.3, f32[5,8,2048]{2,1,0:T(8,128)} %forcing_in.1, f32[2,8,2048]{2,1,0:T(8,128)} %current_in.1, s32[8,2048]{1,0:T(8,128)} %cover_in.1, s32[2,8,2048]{2,1,0:T(8,128)} %targets_in.1, s32[2,8,2048]{2,1,0:T(8,128)} %weights_in.1), custom_call_target="tpu_custom_call" | custom-call | tf_op jit(solution)/shard_map/tiles/pallas_call | solution.py:992
  39.2 0.8 %deliver.1 = (f32[5,8,2048]{2,1,0:T(8,128)}, f32[3,8,2048]{2,1,0:T(8,128)}) custom-call(f32[5,8,2048]{2,1,0:T(8,128)S(1)} %get-tuple-element.6.state, f32[3,8,2048]{2,1,0:T(8,128)S(1)} %get-tuple-element.7.pair), custom_call_target="tpu_custom_call" | custom-call | tf_op jit(solution)/shard_map/deliver/pallas_call | solution.py:968
